TPU v7x, 32 devices: a whole 2x2x4 slice. The times are simulated.
32 devices in a mesh: parts: 2 (over x), dp: 16 (over z, y, core).
Axes of the slice: x: 2, y: 2, z: 4, core: 2. Of those that a mesh axis runs over, the one named last changes fastest.
Arguments:
- train_grads: bfloat16 [16384, 4096], P(('parts', 'dp')), parts along dimension 0, may hold values from -160 to 160
- query_grads: bfloat16 [768, 4096], P(('parts', 'dp')), parts along dimension 0, may hold values from -0.29882812 to 0.29882812
- in_basis: bfloat16 [4, 32, 32], replicated, may hold values from -1 to 1
- out_basis: bfloat16 [4, 32, 32], replicated, may hold values from -1 to 1
- damping: float32 [2], replicated, may hold values from 0.05 to 1
- layer_group: int32 [4], replicated, may hold values from 0 to 1, as said below
Outputs:
- scores: float32 [16384, 384], P(('parts', 'dp')), parts along dimension 0
There are 2 independent parts, one for each index of `parts`. A program takes and returns all parts, laid end to end along the dimension named above; an argument that names none is the same for every part. Nothing has to cross between parts.
Inputs may be any that keep to these rules, and one draw needn't show every extreme that they name: `layer_group`: every group holds at least one layer.
All inputs are finite; a program needn't handle non-finite values.
Results may differ from a plain program's by a relative error of at most 0.0065.
Values may be sent and summed in bfloat16 or wider, within the bound.
No kernel may reach another device: no remote copies, remote signals or barrier semaphores. Data moves between devices by JAX's collectives and lax.ppermute only.
A program may use at most 128 MiB of HBM per device.

v0:
```python
import jax
import jax.numpy as jnp
from jax import lax
from jax.sharding import PartitionSpec as P


def rotate(grads, in_basis, out_basis):
    layers = in_basis.shape[0]
    width = in_basis.shape[1]
    rows = grads.shape[0]
    shaped = grads.reshape(rows, layers, width, width)
    inner = jnp.einsum(
        "tlij,ljb->tlib", shaped, in_basis, preferred_element_type=jnp.float32
    ).astype(jnp.bfloat16)
    outer = jnp.einsum("tlib,lia->tlab", inner, out_basis, preferred_element_type=jnp.float32)
    return outer.reshape(rows, layers * width * width)


def per_device(train_grads, query_grads, in_basis, out_basis, damping, layer_group):
    layers = in_basis.shape[0]
    rotated = rotate(train_grads, in_basis, out_basis)
    totals = lax.psum(jnp.sum(rotated * rotated, axis=0), "dp")
    count = train_grads.shape[0] * lax.axis_size("dp")
    corrected = (totals / count).reshape(layers, -1)
    groups = damping.shape[0]
    pick = (layer_group[:, None] == jnp.arange(groups, dtype=jnp.int32)[None, :]).astype(
        jnp.float32
    )
    per_layer = jnp.sum(pick * damping[None, :], axis=1)
    denominator = (
        corrected + per_layer[:, None] * jnp.mean(corrected, axis=1, keepdims=True)
    ).reshape(-1)
    train_rounded = rotated.astype(jnp.bfloat16)
    prepared = (
        rotate(lax.all_gather(query_grads, "dp", axis=0, tiled=True), in_basis, out_basis)
        / denominator
    ).astype(jnp.bfloat16)
    return lax.dot_general(
        train_rounded, prepared, (((1,), (1,)), ((), ())), preferred_element_type=jnp.float32
    )


def solution(mesh):
    placed = (P(("parts", "dp"), None), P(("parts", "dp"), None), P(), P(), P(), P())
    return jax.shard_map(
        per_device, mesh=mesh, in_specs=placed, out_specs=P(("parts", "dp"), None), check_vma=False
    )
```

profile of v0, /device:TPU:0, one launch (start us, length us, event | category | flops | bytes accessed | tf_op | source)
XLA Modules:
  0.0 106.7 jit_solution(9189898968604316805)
XLA Ops:
  6.5 0.0 copy-start
  6.5 0.0 all-gather.2.cloned.1.call-start
  6.5 0.7 all-gather.2.cloned.1.call-update
  7.3 6.5 %copy.32 = bf16[512,4096]{0,1:T(8,128)(2,1)} copy(bf16[512,4096]{1,0:T(8,128)(2,1)} %param.6) | data formatting | bytes 8388608 | tf_op args[0]
  13.7 0.0 copy-done
  13.7 0.0 copy-start.1
  13.7 3.5 %convert_bitcast_fusion = bf16[512,4,32,32]{0,3,2,1:T(8,128)(2,1)S(1)} fusion(bf16[512,4,32,32]{0,3,2,1:T(8,128)(2,1)} %bitcast.48, bf16[4,32,32]{2,1,0:T(8,128)(2,1)S(1)} %copy-done), kind=kOutput, calls=%fused_computation.8 | convolution fusion | flops 136314880 | bytes 8396800 | tf_op jit(solution)/shard_map/tlij,ljb->tlib/dot_general | solution.py:12
  17.2 0.0 copy-done.1
  17.2 0.0 copy-start.2
  17.2 0.0 copy-start.3
  17.3 4.4 %multiply_reduce_fusion = (f32[4,32,32]{2,1,0:T(8,128)S(1)}, bf16[4,512,32,32]{1,3,2,0:T(8,128)(2,1)}) fusion(bf16[4,32,32]{2,1,0:T(8,128)(2,1)S(1)} %copy-done.1, bf16[512,4,32,32]{0,3,2,1:T(8,128)(2,1)S(1)} %convert_bitcast_fusion), kind=kOutput, calls=%fused_computation | convolution fusion | flops 140505088 | bytes 8413184 | tf_op jit(solution)/shard_map/tlib,lia->tlab/dot_general | solution.py:15
  21.6 0.1 copy.40
  21.7 0.1 reduce_sum.33
  21.8 63.5 %psum.7 = f32[4096]{0:T(1024)S(1)} all-reduce(f32[4096]{0:T(1024)S(1)} %reduce_sum.33), channel_id=1, replica_groups=mesh['parts'=2,'dp'=16] {'dp'}, use_global_device_ids=true, to_apply=%region_1.0 | all-reduce | flops 4096 | bytes 32768 | tf_op jit(solution)/shard_map/psum | solution.py:22
  85.4 0.1 reduce_sum.35
  85.5 0.0 copy-done.2
  85.5 0.0 copy-done.3
  85.5 0.1 fusion.25
  85.6 0.1 broadcast_bitcast_fusion
  85.7 0.1 div.23
  85.7 0.1 copy.41
  85.8 0.0 all-gather.2.cloned.1.call-done
  85.9 3.4 %copy.36 = bf16[384,4096]{0,1:T(8,128)(2,1)S(1)} copy(bf16[384,4096]{1,0:T(8,128)(2,1)} %all-gather.2.cloned.1.call-done) | data formatting | bytes 6291456 | tf_op jit(solution)/shard_map/all_gather | solution.py:35
  89.3 2.7 %convert_bitcast_fusion.1 = bf16[384,4,32,32]{0,3,2,1:T(8,128)(2,1)} fusion(bf16[384,4,32,32]{0,3,2,1:T(8,128)(2,1)S(1)} %bitcast.49, bf16[4,32,32]{2,1,0:T(8,128)(2,1)S(1)} %copy-done), kind=kOutput, calls=%fused_computation.11 | convolution fusion | flops 102236160 | bytes 6299648 | tf_op jit(solution)/shard_map/tlij,ljb->tlib/dot_general | solution.py:12
  92.0 7.9 %fusion.13 = f32[512,384]{1,0:T(8,128)} fusion(f32[4,32,32]{1,2,0:T(8,128)S(1)} %copy.41, bf16[384,4,32,32]{0,3,2,1:T(8,128)(2,1)} %convert_bitcast_fusion.1, bf16[4,512,32,32]{1,3,2,0:T(8,128)(2,1)} %get-tuple-element.6, bf16[4,32,32]{2,1,0:T(8,128)(2,1)S(1)} %copy-done.1), kind=kOutput, calls=%fused_computation.12 | convolution fusion | flops 1714421760 | bytes 8151040 | tf_op jit(solution)/shard_map/dot_general | solution.py:38
  (4 shorter events, 0.0 us)
Async XLA Ops:
  6.5 7.2 %copy-start = (bf16[4,32,32]{2,1,0:T(8,128)(2,1)S(1)}, bf16[4,32,32]{2,1,0:T(8,128)(2,1)}, u32[]{:S(2)}) copy-start(bf16[4,32,32]{2,1,0:T(8,128)(2,1)} %param.8) | copy-start | bytes 24580
  6.5 79.3 %all-gather.2.cloned.1.call-start = ((), (), s32[]{:S(2)}) async-start(), calls=%async_computation | async-start | bytes 3342336 | tf_op jit(solution)/shard_map/all_gather | solution.py:35
  13.7 3.5 %copy-start.1 = (bf16[4,32,32]{2,1,0:T(8,128)(2,1)S(1)}, bf16[4,32,32]{2,1,0:T(8,128)(2,1)}, u32[]{:S(2)}) copy-start(bf16[4,32,32]{2,1,0:T(8,128)(2,1)} %param.9) | copy-start | bytes 24580
  17.2 68.3 %copy-start.2 = (f32[2]{0:T(128)S(1)}, f32[2]{0:T(128)}, u32[]{:S(2)}) copy-start(f32[2]{0:T(128)} %param.10) | copy-start | bytes 28
  17.2 68.2 %copy-start.3 = (s32[4]{0:T(128)S(1)}, s32[4]{0:T(128)}, u32[]{:S(2)}) copy-start(s32[4]{0:T(128)} %param.11) | copy-start | bytes 52
Sparse Core Ops, SparseCore 0:
  9.6 48.3 all-gather.1
where the time goes:
time: 107 us
  blocking collectives  63.5 us (59%)
  matrix products  18.5 us (17%)
  between operations  13.5 us (13%)
  local copies, waits for them, and re-layouts  10.3 us (10%)
    psum x1, blocking collectives, per_device(): totals = lax.psum(jnp.sum(rotated * rotated, axis=0), 'dp')  63.5 us
    dot_general x1, matrix products, per_device(): lax.dot_general(train_rounded, prepared, (((1,), (1,)), ((), ())), prefer...  7.9 us
    unnamed x10, local copies, waits for them, and re-layouts  6.57 us
    dot_general x2, matrix products, rotate(): jnp.einsum('tlij,ljb->tlib', shaped, in_basis, preferred_element_type=jnp...  6.18 us
    dot_general x1, matrix products, rotate(): jnp.einsum('tlib,lia->tlab', inner, out_basis, preferred_element_type=jnp...  4.39 us
    all_gather x1, local copies, waits for them, and re-layouts, per_device(): lax.all_gather(query_grads, 'dp', axis=0, tiled=True)  3.43 us
  transfers between devices with their start and end apart: 1, of which 0 were waited for; matrix products, arithmetic and copies ran while one was open for 14% of the time, Pallas kernels for 0%

commit v1 on v0

v1 whole, which is shorter than its diff:
```python
import functools

import jax
import jax.numpy as jnp
from jax import lax
from jax.experimental import pallas as pl
from jax.experimental.pallas import tpu as pltpu
from jax.sharding import PartitionSpec as P


LANES = 128
MIB = 1024 * 1024
VMEM = pl.BlockSpec(memory_space=pltpu.VMEM)
SMEM = pl.BlockSpec(memory_space=pltpu.SMEM)
HBM = pl.BlockSpec(memory_space=pltpu.HBM)


def stage_matrices(in_ref, out_ref, width):
    layers = in_ref.shape[0]
    group = 2 * LANES // width
    half = LANES // group
    cols, wide = 2 * LANES, half * width

    def iota(shape, dim):
        return lax.broadcasted_iota(jnp.int32, shape, dim)

    spread = iota((width, cols), 1) // group == iota((width, cols), 0)
    repeat = iota((width, wide), 1) % width == iota((width, wide), 0)
    flat_in = in_ref[...].reshape(layers * width, width)
    flat_out = out_ref[...].reshape(layers * width, width)
    wide_in = jnp.dot(flat_in, spread.astype(jnp.bfloat16), preferred_element_type=jnp.float32)
    wide_out = jnp.dot(flat_out, repeat.astype(jnp.bfloat16), preferred_element_type=jnp.float32)
    which = iota((width, cols), 1) % group
    keep = iota((LANES, wide), 0) // group == iota((LANES, wide), 1) // width
    firsts, seconds = [], []
    for l in range(layers):
        rows = wide_in[l * width : (l + 1) * width]
        first = [jnp.where(which == i, rows, 0.0) for i in range(group)]
        firsts.append(jnp.concatenate(first, axis=0).astype(jnp.bfloat16))
        second = []
        for k in range(width // group):
            at = l * width + k * group
            tiled = jnp.concatenate([wide_out[at : at + group]] * half, axis=0)
            second.append(jnp.where(keep, tiled, 0.0))
        seconds.append(jnp.concatenate(second, axis=0).astype(jnp.bfloat16))
    return firsts, seconds


def rotate_layer(x_ref, base, first, second, width):
    cols = 2 * LANES
    inner = []
    for k in range(width * width // cols):
        at = base + k * cols
        inner.append(
            jnp.dot(x_ref[:, at : at + cols], first, preferred_element_type=jnp.float32).astype(
                jnp.bfloat16
            )
        )
    for h in range(2):
        lhs = jnp.concatenate([x[:, h * LANES : (h + 1) * LANES] for x in inner], axis=1)
        yield jnp.dot(lhs, second, preferred_element_type=jnp.float32)


def prepare_kernel(
    layers,
    width,
    q_hbm,
    in_hbm,
    out_hbm,
    x_hbm,
    rot_ref,
    first_ref,
    second_ref,
    held_ref,
    q_ref,
    in_ref,
    out_ref,
    sems,
):
    ends = ((in_hbm, in_ref), (out_hbm, out_ref), (q_hbm, q_ref), (x_hbm, held_ref))
    copies = [pltpu.make_async_copy(a, b, sems.at[i]) for i, (a, b) in enumerate(ends)]
    for copy in copies:
        copy.start()
    for copy in copies[:3]:
        copy.wait()
    firsts, seconds = stage_matrices(in_ref, out_ref, width)
    rows = q_ref.shape[0]
    cols, block = 2 * LANES, width * width
    tiles = block // cols
    inners = []
    for l in range(layers):
        stack = [
            q_ref[:, l * block + k * cols : l * block + (k + 1) * cols].astype(jnp.float32)
            for k in range(tiles)
        ]
        stack = jnp.concatenate(stack, axis=0).astype(jnp.bfloat16)
        inners.append(jnp.dot(stack, firsts[l], preferred_element_type=jnp.float32))
    for l in range(layers):
        halves = [
            jnp.concatenate(
                [
                    inners[l][k * rows : (k + 1) * rows, h * LANES : (h + 1) * LANES]
                    for k in range(tiles)
                ],
                axis=1,
            )
            for h in range(2)
        ]
        lhs = jnp.concatenate(halves, axis=0).astype(jnp.bfloat16)
        rotated = jnp.dot(lhs, seconds[l], preferred_element_type=jnp.float32).astype(jnp.bfloat16)
        at = l * block
        for h in range(2):
            rot_ref[:, at : at + block // 2] = rotated[h * rows : (h + 1) * rows]
            at += block // 2
    for l in range(layers):
        first_ref[l] = firsts[l]
        second_ref[l] = seconds[l]
    copies[3].wait()


def train_kernel(layers, width, x_ref, first_ref, second_ref, rot_ref, sums_ref):
    block = width * width
    for l in range(layers):
        at = l * block
        for rotated in rotate_layer(x_ref, l * block, first_ref[l], second_ref[l], width):
            rot_ref[:, at : at + block // 2] = rotated.astype(jnp.bfloat16)
            sums_ref[:, at : at + block // 2] = jnp.sum(rotated * rotated, axis=0, keepdims=True)
            at += block // 2


def score_kernel(
    layers, steps, rows, train_rows, group_ref, damp_ref, sums_ref, rot_ref, *refs
):
    count = len(steps)
    chips = lax.axis_size("dp") // 2
    me = lax.axis_index("dp")
    chip, mine = me // 2, me % 2
    spot = jnp.where(chip % 2 == 0, chip // 2, chips - 1 - chip // 2)
    pieces, score_ref, scaled = refs[:count], refs[-2], refs[-1]
    block = sums_ref.shape[1] // layers
    spots = []
    for step, twin in steps:
        at = (spot - step + chips) % chips
        first = jnp.where(at < chips // 2, 2 * at, 2 * (chips - 1 - at) + 1) * 2
        spots.append(pl.multiple_of((first + (mine ^ twin)) * rows, 8))

    def fill(l, lanes, slot):
        corrected = sums_ref[:, lanes] / train_rows
        damp = damp_ref[group_ref[l]]
        inverse = 1.0 / (corrected + damp * jnp.mean(corrected, axis=1, keepdims=True))
        for where, piece in zip(spots, pieces):
            scaled[slot, pl.ds(where, rows), :] = piece[:, lanes].astype(jnp.float32) * inverse

    def dot(lanes, right):
        return lax.dot_general(
            rot_ref[:, lanes],
            right.astype(jnp.bfloat16),
            (((1,), (1,)), ((), ())),
            preferred_element_type=jnp.float32,
        )

    if scaled.shape[0] == layers:
        total = None
        for l in range(layers):
            fill(l, slice(l * block, (l + 1) * block), l)
        for l in range(layers):
            product = dot(slice(l * block, (l + 1) * block), scaled[l])
            total = product if total is None else total + product
        score_ref[...] = total
        return

    queries = score_ref.shape[1]
    chunk = next(n for n in (512, 384, 256, 128, queries) if queries % n == 0)
    score_ref[...] = jnp.zeros(score_ref.shape, jnp.float32)

    @pl.loop(0, layers)
    def _(l):
        lanes = pl.ds(pl.multiple_of(l * block, LANES), block)
        fill(l, lanes, 0)

        @pl.loop(0, queries // chunk)
        def _(n):
            at = pl.ds(pl.multiple_of(n * chunk, chunk), chunk)
            score_ref[:, at] += dot(lanes, scaled[0, at, :])


def prepare(queries, in_basis, out_basis, train):
    rows, features = queries.shape
    layers, width, _ = in_basis.shape
    cols = 2 * LANES
    wide = LANES // (cols // width) * width
    return pl.pallas_call(
        functools.partial(prepare_kernel, layers, width),
        in_specs=[HBM] * 4,
        out_specs=[VMEM] * 4,
        out_shape=[
            jax.ShapeDtypeStruct((rows, features), jnp.bfloat16),
            pltpu.VMEM((layers, cols, cols), jnp.bfloat16),
            pltpu.VMEM((layers, wide, wide), jnp.bfloat16),
            pltpu.VMEM(train.shape, train.dtype),
        ],
        scratch_shapes=[
            pltpu.VMEM(queries.shape, queries.dtype),
            pltpu.VMEM(in_basis.shape, in_basis.dtype),
            pltpu.VMEM(out_basis.shape, out_basis.dtype),
            pltpu.SemaphoreType.DMA((4,)),
        ],
        compiler_params=pltpu.CompilerParams(vmem_limit_bytes=16 * MIB),
        cost_estimate=pl.CostEstimate(
            flops=6 * 128 * features * 256, bytes_accessed=2 * train.size, transcendentals=0
        ),
        name="prepare",
    )(*[pltpu.with_memory_space_constraint(x, pltpu.HBM) for x in (queries, in_basis, out_basis, train)])


def rotate_train(train, first, second):
    rows, features = train.shape
    layers = first.shape[0]
    width = 1
    while layers * width * width < features:
        width *= 2
    return pl.pallas_call(
        functools.partial(train_kernel, layers, width),
        in_specs=[VMEM] * 3,
        out_specs=[VMEM] * 2,
        out_shape=[
            pltpu.VMEM((rows, features), jnp.bfloat16),
            jax.ShapeDtypeStruct((1, features), jnp.float32),
        ],
        compiler_params=pltpu.CompilerParams(vmem_limit_bytes=24 * MIB),
        cost_estimate=pl.CostEstimate(
            flops=6 * rows * features * 256, bytes_accessed=4 * rows * features, transcendentals=0
        ),
        name="rotate_train",
    )(train, first, second)


def choose_kernel(even_ref, odd_ref, out_ref):
    core = lax.axis_index("dp") % 2

    @pl.when(core == 0)
    def _():
        out_ref[...] = even_ref[...]

    @pl.when(core == 1)
    def _():
        out_ref[...] = odd_ref[...]


def choose(even, odd):
    return pl.pallas_call(
        choose_kernel,
        in_specs=[VMEM] * 2,
        out_specs=VMEM,
        out_shape=jax.ShapeDtypeStruct(even.shape, even.dtype),
        compiler_params=pltpu.CompilerParams(vmem_limit_bytes=4 * MIB),
        cost_estimate=pl.CostEstimate(
            flops=1000, bytes_accessed=4 * even.size, transcendentals=0
        ),
        name="choose",
    )(even, odd)


def score(steps, layer_group, damping, sums, rotated, pieces, train_rows):
    own, features = rotated.shape
    layers = layer_group.shape[0]
    rows = pieces[0].shape[0]
    count = len(pieces)
    queries = rows * count
    slots = layers if queries <= 512 else 1
    need = 12 * queries * features // layers * slots + 12 * own * queries
    return pl.pallas_call(
        functools.partial(score_kernel, layers, steps, rows, train_rows),
        in_specs=[SMEM, SMEM, VMEM, VMEM] + [VMEM] * count,
        out_specs=VMEM,
        out_shape=jax.ShapeDtypeStruct((own, queries), jnp.float32),
        scratch_shapes=[pltpu.VMEM((slots, queries, features // layers), jnp.float32)],
        compiler_params=pltpu.CompilerParams(vmem_limit_bytes=max(24 * MIB, need)),
        cost_estimate=pl.CostEstimate(
            flops=2 * own * queries * features, bytes_accessed=2 * own * features, transcendentals=0
        ),
        name="score",
    )(layer_group, damping, sums, pltpu.with_memory_space_constraint(rotated, pltpu.VMEM), *pieces)


def ring_order(chips):
    return list(range(0, chips, 2)) + list(range(chips - 1, 0, -2))


def per_device(train_grads, query_grads, in_basis, out_basis, damping, layer_group):
    devices = lax.axis_size("dp")
    chips = devices // 2
    order = ring_order(chips)
    pieces, steps = [], []

    def source(device, step):
        at = order.index(device // 2) - step
        return 2 * order[at % chips] + device % 2

    def ring(step, other=None):
        other = step if other is None else other
        return [(source(d, other if d % 2 else step), d) for d in range(devices)]

    def send(x, pairs):
        return lax.ppermute(x, "dp", pairs)

    def swap(x, bit):
        return send(x, [(i, i ^ bit) for i in range(devices)])

    def keep(chunk, step):
        pieces.extend([chunk, swap(chunk, 1)])
        steps.extend([(step, 0), (step, 1)])

    own, first, second, train = prepare(query_grads, in_basis, out_basis, train_grads)
    rotated, sums = rotate_train(train, first, second)
    far = chips // 2
    ahead = back = own
    keep(own, 0)
    for step in range(1, far):
        ahead = send(ahead, ring(1))
        keep(ahead, step)
        back = send(back, ring(-1))
        keep(back, -step)
    side = choose(ahead, back)
    keep(send(side, ring(1, -1)), far)
    if devices & (devices - 1):
        sums = lax.psum(sums, "dp")
    else:
        bit = 1
        while bit < devices:
            sums = sums + swap(sums, bit)
            bit *= 2

    return score(
        steps, layer_group, damping, sums, rotated, pieces, train_grads.shape[0] * devices
    )


def solution(mesh):
    placed = (P(("parts", "dp"), None), P(("parts", "dp"), None), P(), P(), P(), P())

    return jax.shard_map(
        per_device, mesh=mesh, in_specs=placed, out_specs=P(("parts", "dp"), None), check_vma=False
    )
```

time: 107 us -> 48.3 us (0.45)
  blocking collectives: 63.5 us -> 0 us
  waiting for transfers between devices: 0.73 us -> 22.8 us
  matrix products: 18.5 us -> 0 us
  starting transfers between devices: 0.01 us -> 15.1 us
  between operations: 13.5 us -> 0.06 us
  local copies, waits for them, and re-layouts: 10.3 us -> 0.01 us
  Pallas kernels: 0 us -> 10.1 us
    psum x1 -> x0, blocking collectives: 63.5 us -> none  [per_device(): totals = lax.psum(jnp.sum(rotated * rotated, axis=0), 'dp')]
    ppermute x0 -> x19, waiting for transfers between devices: none -> 22.8 us  [send(): return lax.ppermute(x, 'dp', pairs)]
    dot_general x4 -> x0, matrix products: 18.5 us -> none  [the longest x1 7.9 us: per_device(): lax.dot_general(train_rounded, prepared, (((1,), (1,)), ((), ())), prefer...]
    ppermute x0 -> x19, starting transfers between devices: none -> 15.1 us  [send(): return lax.ppermute(x, 'dp', pairs)]
    pallas_call x0 -> x4, Pallas kernels: none -> 10.1 us  [the longest x1 4.29 us: score(): pl.pallas_call(functools.partial(score_kernel, layers, steps, rows, train...]
    unnamed x10 -> x4, local copies, waits for them, and re-layouts: 6.57 us -> 0.01 us
    all_gather x1 -> x0, local copies, waits for them, and re-layouts: 3.43 us -> none  [per_device(): lax.all_gather(query_grads, 'dp', axis=0, tiled=True)]
  transfers between devices with their start and end apart: 1 -> 19, of which waited for: 0 -> 13; matrix products, arithmetic and copies ran while one was open for 14% -> 0% of each run, Pallas kernels for 0% -> 7%
where the time goes in v1:
time: 48.3 us; the launch traced here: 48.2 us
  waiting for transfers between devices  22.8 us (47%)
  starting transfers between devices  15.1 us (31%)
  Pallas kernels  10.1 us (21%)
    ppermute x19, waiting for transfers between devices, send(): return lax.ppermute(x, 'dp', pairs)  22.8 us
    ppermute x19, starting transfers between devices, send(): return lax.ppermute(x, 'dp', pairs)  15.1 us
    pallas_call x1, Pallas kernels, score(): pl.pallas_call(functools.partial(score_kernel, layers, steps, rows, train...  4.29 us
    pallas_call x1, Pallas kernels, rotate_train(): pl.pallas_call(functools.partial(train_kernel, layers, width), in_specs=[...  3.45 us
    pallas_call x1, Pallas kernels, prepare(): pl.pallas_call(functools.partial(prepare_kernel, layers, width), in_specs...  2.37 us
  transfers between devices with their start and end apart: 19, of which 13 were waited for; matrix products, arithmetic and copies ran while one was open for 0% of the time, Pallas kernels for 7%

profile of v1, /device:TPU:0, one launch (start us, length us, event | category | flops | bytes accessed | tf_op | source)
XLA Modules:
  0.0 48.2 jit_solution(13538027862982740216)
XLA Ops:
  0.0 2.4 %prepare.1 = (bf16[24,4096]{1,0:T(8,128)(2,1)S(1)}, bf16[4,256,256]{2,1,0:T(8,128)(2,1)S(1)}, bf16[4,512,512]{2,1,0:T(8,128)(2,1)S(1)}, bf16[512,4096]{1,0:T(8,128)(2,1)S(1)}) custom-call(bf16[24,4096]{1,0:T(8,128)(2,1)} %q_hbm.1, bf16[4,32,32]{2,1,0:T(8,128)(2,1)} %in_hbm.1, bf16[4,32,32]{2,1,0:T(8,128)(2,1)} %out_hbm.1, bf16[512,4096]{1,0:T(8,128)(2,1)} %x_hbm.1), custom_call_target="tpu_custom_call" | custom-call | flops 805306368 | bytes 4194304 | tf_op jit(solution)/shard_map/prepare/pallas_call | solution.py:192
  2.4 3.0 %collective-permute-start.7 = (bf16[24,4096]{1,0:T(8,128)(2,1)S(1)}, bf16[24,4096]{1,0:T(8,128)(2,1)S(1)}, u32[]{:S(2)}, u32[]{:S(2)}) collective-permute-start(bf16[24,4096]{1,0:T(8,128)(2,1)S(1)} %get-tuple-element.16.refs_0_), channel_id=1, source_target_pairs={{4,0},{5,1},{0,2},{1,3},{8,4},{9,5},{2,6},{3,7},{12,8},{13,9},{6,1... | collective-permute-start | bytes 589832 | tf_op jit(solution)/shard_map/ppermute | solution.py:305
  5.4 0.1 collective-permute-start.5
  5.5 4.8 %collective-permute-done.7.refs_4_ = bf16[24,4096]{1,0:T(8,128)(2,1)S(1)} collective-permute-done((bf16[24,4096]{1,0:T(8,128)(2,1)S(1)}, bf16[24,4096]{1,0:T(8,128)(2,1)S(1)}, u32[]{:S(2)}, u32[]{:S(2)}) %collective-permute-start.7) | collective-permute-done | bytes 196640 | tf_op jit(solution)/shard_map/ppermute | solution.py:305
  10.4 1.7 %collective-permute-start.11 = (bf16[24,4096]{1,0:T(8,128)(2,1)S(1)}, bf16[24,4096]{1,0:T(8,128)(2,1)S(1)}, u32[]{:S(2)}, u32[]{:S(2)}) collective-permute-start(bf16[24,4096]{1,0:T(8,128)(2,1)S(1)} %collective-permute-done.7.refs_4_), channel_id=1, source_target_pairs={{4,0},{5,1},{0,2},{1,3},{8,4},{9,5},{2,6},{3,7},{12,8},{13,9},{6,1... | collective-permute-start | bytes 589832 | tf_op jit(solution)/shard_map/ppermute | solution.py:305
  12.1 0.0 collective-permute-done.5.refs_2_
  12.1 0.3 collective-permute-start.9
  12.4 4.0 %collective-permute-done.11.refs_8_ = bf16[24,4096]{1,0:T(8,128)(2,1)S(1)} collective-permute-done((bf16[24,4096]{1,0:T(8,128)(2,1)S(1)}, bf16[24,4096]{1,0:T(8,128)(2,1)S(1)}, u32[]{:S(2)}, u32[]{:S(2)}) %collective-permute-start.11) | collective-permute-done | bytes 196640 | tf_op jit(solution)/shard_map/ppermute | solution.py:305
  16.5 1.4 %collective-permute-start.15 = (bf16[24,4096]{1,0:T(8,128)(2,1)S(1)}, bf16[24,4096]{1,0:T(8,128)(2,1)S(1)}, u32[]{:S(2)}, u32[]{:S(2)}) collective-permute-start(bf16[24,4096]{1,0:T(8,128)(2,1)S(1)} %collective-permute-done.11.refs_8_), channel_id=1, source_target_pairs={{4,0},{5,1},{0,2},{1,3},{8,4},{9,5},{2,6},{3,7},{12,8},{13,9},{6,1... | collective-permute-start | bytes 589832 | tf_op jit(solution)/shard_map/ppermute | solution.py:305
  17.9 0.0 collective-permute-done.9.refs_6_
  17.9 0.6 %collective-permute-start.13 = (bf16[24,4096]{1,0:T(8,128)(2,1)S(1)}, bf16[24,4096]{1,0:T(8,128)(2,1)S(1)}, u32[]{:S(2)}, u32[]{:S(2)}) collective-permute-start(bf16[24,4096]{1,0:T(8,128)(2,1)S(1)} %collective-permute-done.9.refs_6_), channel_id=1, source_target_pairs={{2,0},{3,1},{6,2},{7,3},{0,4},{1,5},{10,6},{11,7},{4,8},{5,9},{14,... | collective-permute-start | bytes 589832 | tf_op jit(solution)/shard_map/ppermute | solution.py:305
  18.5 0.0 collective-permute-start.4
  18.5 0.5 %collective-permute-start.8 = (bf16[24,4096]{1,0:T(8,128)(2,1)S(1)}, bf16[24,4096]{1,0:T(8,128)(2,1)S(1)}, u32[]{:S(2)}, u32[]{:S(2)}) collective-permute-start(bf16[24,4096]{1,0:T(8,128)(2,1)S(1)} %collective-permute-done.7.refs_4_), channel_id=1, source_target_pairs={{0,1},{1,0},{2,3},{3,2},{4,5},{5,4},{6,7},{7,6},{8,9},{9,8},{10,11... | collective-permute-start | bytes 589832 | tf_op jit(solution)/shard_map/ppermute | solution.py:305
  19.0 0.0 collective-permute-start.6
  19.0 3.1 %collective-permute-done.15.odd_ref.refs_12_ = bf16[24,4096]{1,0:T(8,128)(2,1)S(1)} collective-permute-done((bf16[24,4096]{1,0:T(8,128)(2,1)S(1)}, bf16[24,4096]{1,0:T(8,128)(2,1)S(1)}, u32[]{:S(2)}, u32[]{:S(2)}) %collective-permute-start.15) | collective-permute-done | bytes 196640 | tf_op jit(solution)/shard_map/ppermute | solution.py:305
  22.1 1.4 %collective-permute-done.13.even_ref.refs_10_ = bf16[24,4096]{1,0:T(8,128)(2,1)S(1)} collective-permute-done((bf16[24,4096]{1,0:T(8,128)(2,1)S(1)}, bf16[24,4096]{1,0:T(8,128)(2,1)S(1)}, u32[]{:S(2)}, u32[]{:S(2)}) %collective-permute-start.13) | collective-permute-done | bytes 196640 | tf_op jit(solution)/shard_map/ppermute | solution.py:305
  23.6 0.7 %collective-permute-start.17 = (bf16[24,4096]{1,0:T(8,128)(2,1)S(1)}, bf16[24,4096]{1,0:T(8,128)(2,1)S(1)}, u32[]{:S(2)}, u32[]{:S(2)}) collective-permute-start(bf16[24,4096]{1,0:T(8,128)(2,1)S(1)} %choose.1), channel_id=1, source_target_pairs={{2,0},{5,1},{6,2},{1,3},{0,4},{9,5},{10,6},{3,7},{4,8},{13,9},{14,... | collective-permute-start | bytes 589832 | tf_op jit(solution)/shard_map/ppermute | solution.py:305
  24.2 0.0 copy-start
  24.2 0.0 copy-start.1
  24.2 3.5 %rotate_train.1 = (bf16[512,4096]{1,0:T(8,128)(2,1)S(1)}, f32[1,4096]{1,0:T(1,128)S(1)}) custom-call(bf16[512,4096]{1,0:T(8,128)(2,1)S(1)} %get-tuple-element.11.x_ref, bf16[4,256,256]{2,1,0:T(8,128)(2,1)S(1)} %get-tuple-element.12.first_ref, bf16[4,512,512]{2,1,0:T(8,128)(2,1)S(1)} %get-tuple-element.13.second_ref), custom_call_target="tpu_custom_call" | custom-call | flops 3221225472 | bytes 8388608 | tf_op jit(solution)/shard_map/rotate_train/pallas_call | solution.py:222
  27.7 0.1 collective-permute-start
  27.8 1.2 %collective-permute-done = f32[1,4096]{1,0:T(1,128)S(1)} collective-permute-done((f32[1,4096]{1,0:T(1,128)S(1)}, f32[1,4096]{1,0:T(1,128)S(1)}, u32[]{:S(2)}, u32[]{:S(2)}) %collective-permute-start) | collective-permute-done | bytes 16416 | tf_op jit(solution)/shard_map/ppermute | solution.py:305
  29.0 1.5 %collective-permute-start.1 = (f32[1,4096]{1,0:T(1,128)S(1)}, f32[1,4096]{1,0:T(1,128)S(1)}, u32[]{:S(2)}, u32[]{:S(2)}) collective-permute-start(f32[1,4096]{1,0:T(1,128)S(1)} %add.12), channel_id=1, source_target_pairs={{0,2},{1,3},{2,0},{3,1},{4,6},{5,7},{6,4},{7,5},{8,10},{9,11},{10,... | collective-permute-start | bytes 49160 | tf_op jit(solution)/shard_map/ppermute | solution.py:305
  30.4 2.3 %collective-permute-done.1 = f32[1,4096]{1,0:T(1,128)S(1)} collective-permute-done((f32[1,4096]{1,0:T(1,128)S(1)}, f32[1,4096]{1,0:T(1,128)S(1)}, u32[]{:S(2)}, u32[]{:S(2)}) %collective-permute-start.1) | collective-permute-done | bytes 16416 | tf_op jit(solution)/shard_map/ppermute | solution.py:305
  32.8 1.5 %collective-permute-start.2 = (f32[1,4096]{1,0:T(1,128)S(1)}, f32[1,4096]{1,0:T(1,128)S(1)}, u32[]{:S(2)}, u32[]{:S(2)}) collective-permute-start(f32[1,4096]{1,0:T(1,128)S(1)} %add.13), channel_id=1, source_target_pairs={{0,4},{1,5},{2,6},{3,7},{4,0},{5,1},{6,2},{7,3},{8,12},{9,13},{10,... | collective-permute-start | bytes 49160 | tf_op jit(solution)/shard_map/ppermute | solution.py:305
  34.3 2.3 %collective-permute-done.2 = f32[1,4096]{1,0:T(1,128)S(1)} collective-permute-done((f32[1,4096]{1,0:T(1,128)S(1)}, f32[1,4096]{1,0:T(1,128)S(1)}, u32[]{:S(2)}, u32[]{:S(2)}) %collective-permute-start.2) | collective-permute-done | bytes 16416 | tf_op jit(solution)/shard_map/ppermute | solution.py:305
  36.6 2.5 %collective-permute-start.3 = (f32[1,4096]{1,0:T(1,128)S(1)}, f32[1,4096]{1,0:T(1,128)S(1)}, u32[]{:S(2)}, u32[]{:S(2)}) collective-permute-start(f32[1,4096]{1,0:T(1,128)S(1)} %add.14), channel_id=1, source_target_pairs={{0,8},{1,9},{2,10},{3,11},{4,12},{5,13},{6,14},{7,15},{8,0},{9,1},... | collective-permute-start | bytes 49160 | tf_op jit(solution)/shard_map/ppermute | solution.py:305
  39.2 2.2 %collective-permute-done.3 = f32[1,4096]{1,0:T(1,128)S(1)} collective-permute-done((f32[1,4096]{1,0:T(1,128)S(1)}, f32[1,4096]{1,0:T(1,128)S(1)}, u32[]{:S(2)}, u32[]{:S(2)}) %collective-permute-start.3) | collective-permute-done | bytes 16416 | tf_op jit(solution)/shard_map/ppermute | solution.py:305
  41.3 0.0 collective-permute-start.12
  41.3 0.0 collective-permute-done.4.refs_1_
  41.3 0.5 %collective-permute-start.10 = (bf16[24,4096]{1,0:T(8,128)(2,1)S(1)}, bf16[24,4096]{1,0:T(8,128)(2,1)S(1)}, u32[]{:S(2)}, u32[]{:S(2)}) collective-permute-start(bf16[24,4096]{1,0:T(8,128)(2,1)S(1)} %collective-permute-done.9.refs_6_), channel_id=1, source_target_pairs={{0,1},{1,0},{2,3},{3,2},{4,5},{5,4},{6,7},{7,6},{8,9},{9,8},{10,11... | collective-permute-start | bytes 589832 | tf_op jit(solution)/shard_map/ppermute | solution.py:305
  41.8 0.0 collective-permute-done.8.refs_5_
  41.8 0.1 collective-permute-start.16
  41.9 0.0 collective-permute-done.6.refs_3_
  41.9 0.4 collective-permute-start.14
  42.3 0.0 collective-permute-done.17.refs_14_
  42.4 0.1 collective-permute-start.18
  42.4 0.3 collective-permute-done.12.refs_9_
  42.8 0.3 collective-permute-done.10.refs_7_
  43.0 0.3 collective-permute-done.16.refs_13_
  43.3 0.3 collective-permute-done.14.refs_11_
  43.6 0.3 collective-permute-done.18.refs_15_
  43.9 0.0 copy-done
  43.9 0.0 copy-done.1
  43.9 4.3 %score.1 = f32[512,384]{1,0:T(8,128)} custom-call(s32[4]{0:T(128)S(1)} %copy-done, f32[2]{0:T(128)S(1)} %copy-done.1, f32[1,4096]{1,0:T(1,128)S(1)} %add.15.sums_ref, bf16[512,4096]{1,0:T(8,128)(2,1)S(1)} %get-tuple-element.15.rot_ref, bf16[24,4096]{1,0:T(8,128)(2,1)S(1)} %get-tuple-element.16.refs_0_, bf16[24,4096]{1,0:T(8,128)(2,1)S(1)} %collective-permute-done.4.refs_1_, ...), custom_call_target="tpu_custom_call" | custom-call | flops 1610612736 | bytes 4194304 | tf_op jit(solution)/shard_map/score/pallas_call | solution.py:272
  (5 shorter events, 0.1 us)
Async XLA Ops:
  2.4 8.0 %collective-permute-start.7 = (bf16[24,4096]{1,0:T(8,128)(2,1)S(1)}, bf16[24,4096]{1,0:T(8,128)(2,1)S(1)}, u32[]{:S(2)}, u32[]{:S(2)}) collective-permute-start(bf16[24,4096]{1,0:T(8,128)(2,1)S(1)} %get-tuple-element.16.refs_0_), channel_id=1, source_target_pairs={{4,0},{5,1},{0,2},{1,3},{8,4},{9,5},{2,6},{3,7},{12,8},{13,9},{6,1... | collective-permute-start | bytes 589832 | tf_op jit(solution)/shard_map/ppermute | solution.py:305
  5.4 6.6 %collective-permute-start.5 = (bf16[24,4096]{1,0:T(8,128)(2,1)S(1)}, bf16[24,4096]{1,0:T(8,128)(2,1)S(1)}, u32[]{:S(2)}, u32[]{:S(2)}) collective-permute-start(bf16[24,4096]{1,0:T(8,128)(2,1)S(1)} %get-tuple-element.16.refs_0_), channel_id=1, source_target_pairs={{2,0},{3,1},{6,2},{7,3},{0,4},{1,5},{10,6},{11,7},{4,8},{5,9},{14,... | collective-permute-start | bytes 589832 | tf_op jit(solution)/shard_map/ppermute | solution.py:305
  10.4 6.1 %collective-permute-start.11 = (bf16[24,4096]{1,0:T(8,128)(2,1)S(1)}, bf16[24,4096]{1,0:T(8,128)(2,1)S(1)}, u32[]{:S(2)}, u32[]{:S(2)}) collective-permute-start(bf16[24,4096]{1,0:T(8,128)(2,1)S(1)} %collective-permute-done.7.refs_4_), channel_id=1, source_target_pairs={{4,0},{5,1},{0,2},{1,3},{8,4},{9,5},{2,6},{3,7},{12,8},{13,9},{6,1... | collective-permute-start | bytes 589832 | tf_op jit(solution)/shard_map/ppermute | solution.py:305
  12.1 5.8 %collective-permute-start.9 = (bf16[24,4096]{1,0:T(8,128)(2,1)S(1)}, bf16[24,4096]{1,0:T(8,128)(2,1)S(1)}, u32[]{:S(2)}, u32[]{:S(2)}) collective-permute-start(bf16[24,4096]{1,0:T(8,128)(2,1)S(1)} %collective-permute-done.5.refs_2_), channel_id=1, source_target_pairs={{2,0},{3,1},{6,2},{7,3},{0,4},{1,5},{10,6},{11,7},{4,8},{5,9},{14,... | collective-permute-start | bytes 589832 | tf_op jit(solution)/shard_map/ppermute | solution.py:305
  16.5 5.7 %collective-permute-start.15 = (bf16[24,4096]{1,0:T(8,128)(2,1)S(1)}, bf16[24,4096]{1,0:T(8,128)(2,1)S(1)}, u32[]{:S(2)}, u32[]{:S(2)}) collective-permute-start(bf16[24,4096]{1,0:T(8,128)(2,1)S(1)} %collective-permute-done.11.refs_8_), channel_id=1, source_target_pairs={{4,0},{5,1},{0,2},{1,3},{8,4},{9,5},{2,6},{3,7},{12,8},{13,9},{6,1... | collective-permute-start | bytes 589832 | tf_op jit(solution)/shard_map/ppermute | solution.py:305
  17.9 5.7 %collective-permute-start.13 = (bf16[24,4096]{1,0:T(8,128)(2,1)S(1)}, bf16[24,4096]{1,0:T(8,128)(2,1)S(1)}, u32[]{:S(2)}, u32[]{:S(2)}) collective-permute-start(bf16[24,4096]{1,0:T(8,128)(2,1)S(1)} %collective-permute-done.9.refs_6_), channel_id=1, source_target_pairs={{2,0},{3,1},{6,2},{7,3},{0,4},{1,5},{10,6},{11,7},{4,8},{5,9},{14,... | collective-permute-start | bytes 589832 | tf_op jit(solution)/shard_map/ppermute | solution.py:305
  18.5 22.8 %collective-permute-start.4 = (bf16[24,4096]{1,0:T(8,128)(2,1)S(1)}, bf16[24,4096]{1,0:T(8,128)(2,1)S(1)}, u32[]{:S(2)}, u32[]{:S(2)}) collective-permute-start(bf16[24,4096]{1,0:T(8,128)(2,1)S(1)} %get-tuple-element.16.refs_0_), channel_id=1, source_target_pairs={{0,1},{1,0},{2,3},{3,2},{4,5},{5,4},{6,7},{7,6},{8,9},{9,8},{10,11... | collective-permute-start | bytes 589832 | tf_op jit(solution)/shard_map/ppermute | solution.py:305
  18.5 23.3 %collective-permute-start.8 = (bf16[24,4096]{1,0:T(8,128)(2,1)S(1)}, bf16[24,4096]{1,0:T(8,128)(2,1)S(1)}, u32[]{:S(2)}, u32[]{:S(2)}) collective-permute-start(bf16[24,4096]{1,0:T(8,128)(2,1)S(1)} %collective-permute-done.7.refs_4_), channel_id=1, source_target_pairs={{0,1},{1,0},{2,3},{3,2},{4,5},{5,4},{6,7},{7,6},{8,9},{9,8},{10,11... | collective-permute-start | bytes 589832 | tf_op jit(solution)/shard_map/ppermute | solution.py:305
  19.0 22.9 %collective-permute-start.6 = (bf16[24,4096]{1,0:T(8,128)(2,1)S(1)}, bf16[24,4096]{1,0:T(8,128)(2,1)S(1)}, u32[]{:S(2)}, u32[]{:S(2)}) collective-permute-start(bf16[24,4096]{1,0:T(8,128)(2,1)S(1)} %collective-permute-done.5.refs_2_), channel_id=1, source_target_pairs={{0,1},{1,0},{2,3},{3,2},{4,5},{5,4},{6,7},{7,6},{8,9},{9,8},{10,11... | collective-permute-start | bytes 589832 | tf_op jit(solution)/shard_map/ppermute | solution.py:305
  23.6 18.8 %collective-permute-start.17 = (bf16[24,4096]{1,0:T(8,128)(2,1)S(1)}, bf16[24,4096]{1,0:T(8,128)(2,1)S(1)}, u32[]{:S(2)}, u32[]{:S(2)}) collective-permute-start(bf16[24,4096]{1,0:T(8,128)(2,1)S(1)} %choose.1), channel_id=1, source_target_pairs={{2,0},{5,1},{6,2},{1,3},{0,4},{9,5},{10,6},{3,7},{4,8},{13,9},{14,... | collective-permute-start | bytes 589832 | tf_op jit(solution)/shard_map/ppermute | solution.py:305
  24.2 19.7 %copy-start = (s32[4]{0:T(128)S(1)}, s32[4]{0:T(128)}, u32[]{:S(2)}) copy-start(s32[4]{0:T(128)} %group_ref.1) | copy-start | bytes 52
  24.2 19.7 %copy-start.1 = (f32[2]{0:T(128)S(1)}, f32[2]{0:T(128)}, u32[]{:S(2)}) copy-start(f32[2]{0:T(128)} %damp_ref.1) | copy-start | bytes 28
  27.7 1.2 %collective-permute-start = (f32[1,4096]{1,0:T(1,128)S(1)}, f32[1,4096]{1,0:T(1,128)S(1)}, u32[]{:S(2)}, u32[]{:S(2)}) collective-permute-start(f32[1,4096]{1,0:T(1,128)S(1)} %get-tuple-element.14), channel_id=1, source_target_pairs={{0,1},{1,0},{2,3},{3,2},{4,5},{5,4},{6,7},{7,6},{8,9},{9,8},{10,11... | collective-permute-start | bytes 49160 | tf_op jit(solution)/shard_map/ppermute | solution.py:305
  29.0 3.8 %collective-permute-start.1 = (f32[1,4096]{1,0:T(1,128)S(1)}, f32[1,4096]{1,0:T(1,128)S(1)}, u32[]{:S(2)}, u32[]{:S(2)}) collective-permute-start(f32[1,4096]{1,0:T(1,128)S(1)} %add.12), channel_id=1, source_target_pairs={{0,2},{1,3},{2,0},{3,1},{4,6},{5,7},{6,4},{7,5},{8,10},{9,11},{10,... | collective-permute-start | bytes 49160 | tf_op jit(solution)/shard_map/ppermute | solution.py:305
  32.8 3.8 %collective-permute-start.2 = (f32[1,4096]{1,0:T(1,128)S(1)}, f32[1,4096]{1,0:T(1,128)S(1)}, u32[]{:S(2)}, u32[]{:S(2)}) collective-permute-start(f32[1,4096]{1,0:T(1,128)S(1)} %add.13), channel_id=1, source_target_pairs={{0,4},{1,5},{2,6},{3,7},{4,0},{5,1},{6,2},{7,3},{8,12},{9,13},{10,... | collective-permute-start | bytes 49160 | tf_op jit(solution)/shard_map/ppermute | solution.py:305
  36.6 4.7 %collective-permute-start.3 = (f32[1,4096]{1,0:T(1,128)S(1)}, f32[1,4096]{1,0:T(1,128)S(1)}, u32[]{:S(2)}, u32[]{:S(2)}) collective-permute-start(f32[1,4096]{1,0:T(1,128)S(1)} %add.14), channel_id=1, source_target_pairs={{0,8},{1,9},{2,10},{3,11},{4,12},{5,13},{6,14},{7,15},{8,0},{9,1},... | collective-permute-start | bytes 49160 | tf_op jit(solution)/shard_map/ppermute | solution.py:305
  41.3 1.4 %collective-permute-start.12 = (bf16[24,4096]{1,0:T(8,128)(2,1)S(1)}, bf16[24,4096]{1,0:T(8,128)(2,1)S(1)}, u32[]{:S(2)}, u32[]{:S(2)}) collective-permute-start(bf16[24,4096]{1,0:T(8,128)(2,1)S(1)} %collective-permute-done.11.refs_8_), channel_id=1, source_target_pairs={{0,1},{1,0},{2,3},{3,2},{4,5},{5,4},{6,7},{7,6},{8,9},{9,8},{10,11... | collective-permute-start | bytes 589832 | tf_op jit(solution)/shard_map/ppermute | solution.py:305
  41.3 1.7 %collective-permute-start.10 = (bf16[24,4096]{1,0:T(8,128)(2,1)S(1)}, bf16[24,4096]{1,0:T(8,128)(2,1)S(1)}, u32[]{:S(2)}, u32[]{:S(2)}) collective-permute-start(bf16[24,4096]{1,0:T(8,128)(2,1)S(1)} %collective-permute-done.9.refs_6_), channel_id=1, source_target_pairs={{0,1},{1,0},{2,3},{3,2},{4,5},{5,4},{6,7},{7,6},{8,9},{9,8},{10,11... | collective-permute-start | bytes 589832 | tf_op jit(solution)/shard_map/ppermute | solution.py:305
  41.8 1.5 %collective-permute-start.16 = (bf16[24,4096]{1,0:T(8,128)(2,1)S(1)}, bf16[24,4096]{1,0:T(8,128)(2,1)S(1)}, u32[]{:S(2)}, u32[]{:S(2)}) collective-permute-start(bf16[24,4096]{1,0:T(8,128)(2,1)S(1)} %collective-permute-done.15.odd_ref.refs_12_), channel_id=1, source_target_pairs={{0,1},{1,0},{2,3},{3,2},{4,5},{5,4},{6,7},{7,6},{8,9},{9,8},{10,11... | collective-permute-start | bytes 589832 | tf_op jit(solution)/shard_map/ppermute | solution.py:305
  41.9 1.7 %collective-permute-start.14 = (bf16[24,4096]{1,0:T(8,128)(2,1)S(1)}, bf16[24,4096]{1,0:T(8,128)(2,1)S(1)}, u32[]{:S(2)}, u32[]{:S(2)}) collective-permute-start(bf16[24,4096]{1,0:T(8,128)(2,1)S(1)} %collective-permute-done.13.even_ref.refs_10_), channel_id=1, source_target_pairs={{0,1},{1,0},{2,3},{3,2},{4,5},{5,4},{6,7},{7,6},{8,9},{9,8},{10,11... | collective-permute-start | bytes 589832 | tf_op jit(solution)/shard_map/ppermute | solution.py:305
  42.4 1.5 %collective-permute-start.18 = (bf16[24,4096]{1,0:T(8,128)(2,1)S(1)}, bf16[24,4096]{1,0:T(8,128)(2,1)S(1)}, u32[]{:S(2)}, u32[]{:S(2)}) collective-permute-start(bf16[24,4096]{1,0:T(8,128)(2,1)S(1)} %collective-permute-done.17.refs_14_), channel_id=1, source_target_pairs={{0,1},{1,0},{2,3},{3,2},{4,5},{5,4},{6,7},{7,6},{8,9},{9,8},{10,11... | collective-permute-start | bytes 589832 | tf_op jit(solution)/shard_map/ppermute | solution.py:305

commit v2 on v1

--- a/solution.py
+++ b/solution.py
@@ -77,7 +77,8 @@
     out_ref,
     sems,
 ):
-    ends = ((in_hbm, in_ref), (out_hbm, out_ref), (q_hbm, q_ref), (x_hbm, held_ref))
+    held = x_hbm.at[:, pl.ds(0, held_ref.shape[1])]
+    ends = ((in_hbm, in_ref), (out_hbm, out_ref), (q_hbm, q_ref), (held, held_ref))
     copies = [pltpu.make_async_copy(a, b, sems.at[i]) for i, (a, b) in enumerate(ends)]
     for copy in copies:
         copy.start()
@@ -118,25 +119,45 @@
     copies[3].wait()
 
 
-def train_kernel(layers, width, x_ref, first_ref, second_ref, rot_ref, sums_ref):
+def train_kernel(
+    layers,
+    width,
+    early,
+    x_hbm,
+    held_ref,
+    first_ref,
+    second_ref,
+    rot_ref,
+    sums_ref,
+    late_ref,
+    sems,
+):
     block = width * width
+    copies = []
+    for l in range(early, layers):
+        source = x_hbm.at[:, pl.ds(l * block, block)]
+        copies.append(pltpu.make_async_copy(source, late_ref.at[l - early], sems.at[l - early]))
+        copies[-1].start()
     for l in range(layers):
         at = l * block
-        for rotated in rotate_layer(x_ref, l * block, first_ref[l], second_ref[l], width):
+        if l >= early:
+            copies[l - early].wait()
+        x_ref, base = (held_ref, at) if l < early else (late_ref.at[l - early], 0)
+        for rotated in rotate_layer(x_ref, base, first_ref[l], second_ref[l], width):
             rot_ref[:, at : at + block // 2] = rotated.astype(jnp.bfloat16)
             sums_ref[:, at : at + block // 2] = jnp.sum(rotated * rotated, axis=0, keepdims=True)
             at += block // 2
 
 
 def score_kernel(
-    layers, steps, rows, train_rows, group_ref, damp_ref, sums_ref, rot_ref, *refs
+    layers, steps, rows, train_rows, group_ref, damping_ref, sums_ref, rot_ref, *refs
 ):
     count = len(steps)
     chips = lax.axis_size("dp") // 2
     me = lax.axis_index("dp")
     chip, mine = me // 2, me % 2
     spot = jnp.where(chip % 2 == 0, chip // 2, chips - 1 - chip // 2)
-    pieces, score_ref, scaled = refs[:count], refs[-2], refs[-1]
+    pieces, score_ref, scaled = refs[:count], refs[count], refs[count + 1 :]
     block = sums_ref.shape[1] // layers
     spots = []
     for step, twin in steps:
@@ -145,11 +166,15 @@
         spots.append(pl.multiple_of((first + (mine ^ twin)) * rows, 8))
 
     def fill(l, lanes, slot):
+        numbers = lax.broadcasted_iota(jnp.int32, group_ref.shape, 1)
+        group = jnp.sum(jnp.where(numbers == l, group_ref[...], 0), axis=1, keepdims=True)
+        damps = lax.broadcasted_iota(jnp.int32, damping_ref.shape, 1) == group
+        damp = jnp.sum(jnp.where(damps, damping_ref[...], 0.0), axis=1, keepdims=True)
         corrected = sums_ref[:, lanes] / train_rows
-        damp = damp_ref[group_ref[l]]
-        inverse = 1.0 / (corrected + damp * jnp.mean(corrected, axis=1, keepdims=True))
+        mean = jnp.mean(corrected, axis=1, keepdims=True)
+        inverse = 1.0 / (corrected + damp * mean)
         for where, piece in zip(spots, pieces):
-            scaled[slot, pl.ds(where, rows), :] = piece[:, lanes].astype(jnp.float32) * inverse
+            scaled[slot][pl.ds(where, rows), :] = piece[:, lanes].astype(jnp.float32) * inverse
 
     def dot(lanes, right):
         return lax.dot_general(
@@ -159,12 +184,12 @@
             preferred_element_type=jnp.float32,
         )
 
-    if scaled.shape[0] == layers:
+    if len(scaled) == layers:
         total = None
         for l in range(layers):
             fill(l, slice(l * block, (l + 1) * block), l)
         for l in range(layers):
-            product = dot(slice(l * block, (l + 1) * block), scaled[l])
+            product = dot(slice(l * block, (l + 1) * block), scaled[l][...])
             total = product if total is None else total + product
         score_ref[...] = total
         return
@@ -181,10 +206,10 @@
         @pl.loop(0, queries // chunk)
         def _(n):
             at = pl.ds(pl.multiple_of(n * chunk, chunk), chunk)
-            score_ref[:, at] += dot(lanes, scaled[0, at, :])
-
-
-def prepare(queries, in_basis, out_basis, train):
+            score_ref[:, at] += dot(lanes, scaled[0][at, :])
+
+
+def prepare(queries, in_basis, out_basis, train, early):
     rows, features = queries.shape
     layers, width, _ = in_basis.shape
     cols = 2 * LANES
@@ -197,7 +222,7 @@
             jax.ShapeDtypeStruct((rows, features), jnp.bfloat16),
             pltpu.VMEM((layers, cols, cols), jnp.bfloat16),
             pltpu.VMEM((layers, wide, wide), jnp.bfloat16),
-            pltpu.VMEM(train.shape, train.dtype),
+            pltpu.VMEM((train.shape[0], features // layers * early), train.dtype),
         ],
         scratch_shapes=[
             pltpu.VMEM(queries.shape, queries.dtype),
@@ -213,26 +238,30 @@
     )(*[pltpu.with_memory_space_constraint(x, pltpu.HBM) for x in (queries, in_basis, out_basis, train)])
 
 
-def rotate_train(train, first, second):
+def rotate_train(train, held, first, second, width):
     rows, features = train.shape
     layers = first.shape[0]
-    width = 1
-    while layers * width * width < features:
-        width *= 2
+    block = features // layers
+    early = held.shape[1] // block
+    late = layers - early
     return pl.pallas_call(
-        functools.partial(train_kernel, layers, width),
-        in_specs=[VMEM] * 3,
+        functools.partial(train_kernel, layers, width, early),
+        in_specs=[HBM] + [VMEM] * 3,
         out_specs=[VMEM] * 2,
         out_shape=[
             pltpu.VMEM((rows, features), jnp.bfloat16),
             jax.ShapeDtypeStruct((1, features), jnp.float32),
+        ],
+        scratch_shapes=[
+            pltpu.VMEM((max(late, 1), rows, block), train.dtype),
+            pltpu.SemaphoreType.DMA((max(late, 1),)),
         ],
         compiler_params=pltpu.CompilerParams(vmem_limit_bytes=24 * MIB),
         cost_estimate=pl.CostEstimate(
             flops=6 * rows * features * 256, bytes_accessed=4 * rows * features, transcendentals=0
         ),
         name="rotate_train",
-    )(train, first, second)
+    )(pltpu.with_memory_space_constraint(train, pltpu.HBM), held, first, second)
 
 
 def choose_kernel(even_ref, odd_ref, out_ref):
@@ -271,16 +300,16 @@
     need = 12 * queries * features // layers * slots + 12 * own * queries
     return pl.pallas_call(
         functools.partial(score_kernel, layers, steps, rows, train_rows),
-        in_specs=[SMEM, SMEM, VMEM, VMEM] + [VMEM] * count,
+        in_specs=[VMEM] * (4 + count),
         out_specs=VMEM,
         out_shape=jax.ShapeDtypeStruct((own, queries), jnp.float32),
-        scratch_shapes=[pltpu.VMEM((slots, queries, features // layers), jnp.float32)],
+        scratch_shapes=[pltpu.VMEM((queries, features // layers), jnp.float32)] * slots,
         compiler_params=pltpu.CompilerParams(vmem_limit_bytes=max(24 * MIB, need)),
         cost_estimate=pl.CostEstimate(
             flops=2 * own * queries * features, bytes_accessed=2 * own * features, transcendentals=0
         ),
         name="score",
-    )(layer_group, damping, sums, pltpu.with_memory_space_constraint(rotated, pltpu.VMEM), *pieces)
+    )(layer_group[None], damping[None], sums, pltpu.with_memory_space_constraint(rotated, pltpu.VMEM), *pieces)
 
 
 def ring_order(chips):
@@ -311,8 +340,10 @@
         pieces.extend([chunk, swap(chunk, 1)])
         steps.extend([(step, 0), (step, 1)])
 
-    own, first, second, train = prepare(query_grads, in_basis, out_basis, train_grads)
-    rotated, sums = rotate_train(train, first, second)
+    layers, width, _ = in_basis.shape
+    early = (layers + 1) // 2
+    own, first, second, held = prepare(query_grads, in_basis, out_basis, train_grads, early)
+    rotated, sums = rotate_train(train_grads, held, first, second, width)
     far = chips // 2
     ahead = back = own
     keep(own, 0)

time: 48.3 us -> 47.5 us (0.983)
  Pallas kernels: 10.1 us -> 9.34 us
    pallas_call x1, Pallas kernels: 4.29 us -> 3.64 us  [score(): pl.pallas_call(functools.partial(score_kernel, layers, steps, rows, train...]
    pallas_call x1, Pallas kernels: 2.37 us -> 1.85 us  [prepare(): pl.pallas_call(functools.partial(prepare_kernel, layers, width), in_specs...]
  transfers between devices with their start and end apart: 19 -> 19, of which waited for: 13 -> 13; matrix products, arithmetic and copies ran while one was open for 0% -> 0% of each run, Pallas kernels for 7% -> 8%
where the time goes in v2:
time: 47.5 us; the launch traced here: 47.4 us
  waiting for transfers between devices  22.8 us (48%)
  starting transfers between devices  15.1 us (32%)
  Pallas kernels  9.34 us (20%)
    ppermute x19, waiting for transfers between devices, send(): return lax.ppermute(x, 'dp', pairs)  22.8 us
    ppermute x19, starting transfers between devices, send(): return lax.ppermute(x, 'dp', pairs)  15.1 us
    pallas_call x1, Pallas kernels, rotate_train(): pl.pallas_call(functools.partial(train_kernel, layers, width, early), in_...  3.83 us
    pallas_call x1, Pallas kernels, score(): pl.pallas_call(functools.partial(score_kernel, layers, steps, rows, train...  3.64 us
    pallas_call x1, Pallas kernels, prepare(): pl.pallas_call(functools.partial(prepare_kernel, layers, width), in_specs...  1.85 us
  transfers between devices with their start and end apart: 19, of which 13 were waited for; matrix products, arithmetic and copies ran while one was open for 0% of the time, Pallas kernels for 8%

profile of v2, /device:TPU:0, one launch (start us, length us, event | category | flops | bytes accessed | tf_op | source)
XLA Modules:
  0.0 47.4 jit_solution(1218094694675048952)
XLA Ops:
  0.0 1.9 %prepare.1 = (bf16[24,4096]{1,0:T(8,128)(2,1)S(1)}, bf16[4,256,256]{2,1,0:T(8,128)(2,1)S(1)}, bf16[4,512,512]{2,1,0:T(8,128)(2,1)S(1)}, bf16[512,2048]{1,0:T(8,128)(2,1)S(1)}) custom-call(bf16[24,4096]{1,0:T(8,128)(2,1)} %q_hbm.1, bf16[4,32,32]{2,1,0:T(8,128)(2,1)} %in_hbm.1, bf16[4,32,32]{2,1,0:T(8,128)(2,1)} %out_hbm.1, bf16[512,4096]{1,0:T(8,128)(2,1)} %x_hbm.3), custom_call_target="tpu_custom_call" | custom-call | flops 805306368 | bytes 4194304 | tf_op jit(solution)/shard_map/prepare/pallas_call | solution.py:217
  1.9 3.0 %collective-permute-start.7 = (bf16[24,4096]{1,0:T(8,128)(2,1)S(1)}, bf16[24,4096]{1,0:T(8,128)(2,1)S(1)}, u32[]{:S(2)}, u32[]{:S(2)}) collective-permute-start(bf16[24,4096]{1,0:T(8,128)(2,1)S(1)} %get-tuple-element.16.refs_0_), channel_id=1, source_target_pairs={{4,0},{5,1},{0,2},{1,3},{8,4},{9,5},{2,6},{3,7},{12,8},{13,9},{6,1... | collective-permute-start | bytes 589832 | tf_op jit(solution)/shard_map/ppermute | solution.py:334
  4.9 0.1 collective-permute-start.5
  5.0 4.8 %collective-permute-done.7.refs_4_ = bf16[24,4096]{1,0:T(8,128)(2,1)S(1)} collective-permute-done((bf16[24,4096]{1,0:T(8,128)(2,1)S(1)}, bf16[24,4096]{1,0:T(8,128)(2,1)S(1)}, u32[]{:S(2)}, u32[]{:S(2)}) %collective-permute-start.7) | collective-permute-done | bytes 196640 | tf_op jit(solution)/shard_map/ppermute | solution.py:334
  9.9 1.7 %collective-permute-start.11 = (bf16[24,4096]{1,0:T(8,128)(2,1)S(1)}, bf16[24,4096]{1,0:T(8,128)(2,1)S(1)}, u32[]{:S(2)}, u32[]{:S(2)}) collective-permute-start(bf16[24,4096]{1,0:T(8,128)(2,1)S(1)} %collective-permute-done.7.refs_4_), channel_id=1, source_target_pairs={{4,0},{5,1},{0,2},{1,3},{8,4},{9,5},{2,6},{3,7},{12,8},{13,9},{6,1... | collective-permute-start | bytes 589832 | tf_op jit(solution)/shard_map/ppermute | solution.py:334
  11.6 0.0 collective-permute-done.5.refs_2_
  11.6 0.3 collective-permute-start.9
  11.9 4.0 %collective-permute-done.11.refs_8_ = bf16[24,4096]{1,0:T(8,128)(2,1)S(1)} collective-permute-done((bf16[24,4096]{1,0:T(8,128)(2,1)S(1)}, bf16[24,4096]{1,0:T(8,128)(2,1)S(1)}, u32[]{:S(2)}, u32[]{:S(2)}) %collective-permute-start.11) | collective-permute-done | bytes 196640 | tf_op jit(solution)/shard_map/ppermute | solution.py:334
  15.9 1.4 %collective-permute-start.15 = (bf16[24,4096]{1,0:T(8,128)(2,1)S(1)}, bf16[24,4096]{1,0:T(8,128)(2,1)S(1)}, u32[]{:S(2)}, u32[]{:S(2)}) collective-permute-start(bf16[24,4096]{1,0:T(8,128)(2,1)S(1)} %collective-permute-done.11.refs_8_), channel_id=1, source_target_pairs={{4,0},{5,1},{0,2},{1,3},{8,4},{9,5},{2,6},{3,7},{12,8},{13,9},{6,1... | collective-permute-start | bytes 589832 | tf_op jit(solution)/shard_map/ppermute | solution.py:334
  17.3 0.0 collective-permute-done.9.refs_6_
  17.3 0.6 %collective-permute-start.13 = (bf16[24,4096]{1,0:T(8,128)(2,1)S(1)}, bf16[24,4096]{1,0:T(8,128)(2,1)S(1)}, u32[]{:S(2)}, u32[]{:S(2)}) collective-permute-start(bf16[24,4096]{1,0:T(8,128)(2,1)S(1)} %collective-permute-done.9.refs_6_), channel_id=1, source_target_pairs={{2,0},{3,1},{6,2},{7,3},{0,4},{1,5},{10,6},{11,7},{4,8},{5,9},{14,... | collective-permute-start | bytes 589832 | tf_op jit(solution)/shard_map/ppermute | solution.py:334
  18.0 0.0 collective-permute-start.4
  18.0 0.5 %collective-permute-start.8 = (bf16[24,4096]{1,0:T(8,128)(2,1)S(1)}, bf16[24,4096]{1,0:T(8,128)(2,1)S(1)}, u32[]{:S(2)}, u32[]{:S(2)}) collective-permute-start(bf16[24,4096]{1,0:T(8,128)(2,1)S(1)} %collective-permute-done.7.refs_4_), channel_id=1, source_target_pairs={{0,1},{1,0},{2,3},{3,2},{4,5},{5,4},{6,7},{7,6},{8,9},{9,8},{10,11... | collective-permute-start | bytes 589832 | tf_op jit(solution)/shard_map/ppermute | solution.py:334
  18.5 0.0 collective-permute-start.6
  18.5 3.1 %collective-permute-done.15.odd_ref.refs_12_ = bf16[24,4096]{1,0:T(8,128)(2,1)S(1)} collective-permute-done((bf16[24,4096]{1,0:T(8,128)(2,1)S(1)}, bf16[24,4096]{1,0:T(8,128)(2,1)S(1)}, u32[]{:S(2)}, u32[]{:S(2)}) %collective-permute-start.15) | collective-permute-done | bytes 196640 | tf_op jit(solution)/shard_map/ppermute | solution.py:334
  21.6 1.4 %collective-permute-done.13.even_ref.refs_10_ = bf16[24,4096]{1,0:T(8,128)(2,1)S(1)} collective-permute-done((bf16[24,4096]{1,0:T(8,128)(2,1)S(1)}, bf16[24,4096]{1,0:T(8,128)(2,1)S(1)}, u32[]{:S(2)}, u32[]{:S(2)}) %collective-permute-start.13) | collective-permute-done | bytes 196640 | tf_op jit(solution)/shard_map/ppermute | solution.py:334
  23.0 0.7 %collective-permute-start.17 = (bf16[24,4096]{1,0:T(8,128)(2,1)S(1)}, bf16[24,4096]{1,0:T(8,128)(2,1)S(1)}, u32[]{:S(2)}, u32[]{:S(2)}) collective-permute-start(bf16[24,4096]{1,0:T(8,128)(2,1)S(1)} %choose.1), channel_id=1, source_target_pairs={{2,0},{5,1},{6,2},{1,3},{0,4},{9,5},{10,6},{3,7},{4,8},{13,9},{14,... | collective-permute-start | bytes 589832 | tf_op jit(solution)/shard_map/ppermute | solution.py:334
  23.7 0.0 copy-start
  23.7 0.0 copy-start.1
  23.7 3.8 %rotate_train.1 = (bf16[512,4096]{1,0:T(8,128)(2,1)S(1)}, f32[1,4096]{1,0:T(1,128)S(1)}) custom-call(bf16[512,4096]{1,0:T(8,128)(2,1)} %x_hbm.3, bf16[512,2048]{1,0:T(8,128)(2,1)S(1)} %get-tuple-element.11.held_ref, bf16[4,256,256]{2,1,0:T(8,128)(2,1)S(1)} %get-tuple-element.12.first_ref, bf16[4,512,512]{2,1,0:T(8,128)(2,1)S(1)} %get-tuple-element.13.second_ref), custom_call_target="tpu_custom_call" | custom-call | flops 3221225472 | bytes 8388608 | tf_op jit(solution)/shard_map/rotate_train/pallas_call | solution.py:247
  27.6 0.1 collective-permute-start
  27.6 1.2 %collective-permute-done = f32[1,4096]{1,0:T(1,128)S(1)} collective-permute-done((f32[1,4096]{1,0:T(1,128)S(1)}, f32[1,4096]{1,0:T(1,128)S(1)}, u32[]{:S(2)}, u32[]{:S(2)}) %collective-permute-start) | collective-permute-done | bytes 16416 | tf_op jit(solution)/shard_map/ppermute | solution.py:334
  28.8 1.5 %collective-permute-start.1 = (f32[1,4096]{1,0:T(1,128)S(1)}, f32[1,4096]{1,0:T(1,128)S(1)}, u32[]{:S(2)}, u32[]{:S(2)}) collective-permute-start(f32[1,4096]{1,0:T(1,128)S(1)} %add.12), channel_id=1, source_target_pairs={{0,2},{1,3},{2,0},{3,1},{4,6},{5,7},{6,4},{7,5},{8,10},{9,11},{10,... | collective-permute-start | bytes 49160 | tf_op jit(solution)/shard_map/ppermute | solution.py:334
  30.3 2.3 %collective-permute-done.1 = f32[1,4096]{1,0:T(1,128)S(1)} collective-permute-done((f32[1,4096]{1,0:T(1,128)S(1)}, f32[1,4096]{1,0:T(1,128)S(1)}, u32[]{:S(2)}, u32[]{:S(2)}) %collective-permute-start.1) | collective-permute-done | bytes 16416 | tf_op jit(solution)/shard_map/ppermute | solution.py:334
  32.7 1.5 %collective-permute-start.2 = (f32[1,4096]{1,0:T(1,128)S(1)}, f32[1,4096]{1,0:T(1,128)S(1)}, u32[]{:S(2)}, u32[]{:S(2)}) collective-permute-start(f32[1,4096]{1,0:T(1,128)S(1)} %add.13), channel_id=1, source_target_pairs={{0,4},{1,5},{2,6},{3,7},{4,0},{5,1},{6,2},{7,3},{8,12},{9,13},{10,... | collective-permute-start | bytes 49160 | tf_op jit(solution)/shard_map/ppermute | solution.py:334
  34.2 2.3 %collective-permute-done.2 = f32[1,4096]{1,0:T(1,128)S(1)} collective-permute-done((f32[1,4096]{1,0:T(1,128)S(1)}, f32[1,4096]{1,0:T(1,128)S(1)}, u32[]{:S(2)}, u32[]{:S(2)}) %collective-permute-start.2) | collective-permute-done | bytes 16416 | tf_op jit(solution)/shard_map/ppermute | solution.py:334
  36.5 2.5 %collective-permute-start.3 = (f32[1,4096]{1,0:T(1,128)S(1)}, f32[1,4096]{1,0:T(1,128)S(1)}, u32[]{:S(2)}, u32[]{:S(2)}) collective-permute-start(f32[1,4096]{1,0:T(1,128)S(1)} %add.14), channel_id=1, source_target_pairs={{0,8},{1,9},{2,10},{3,11},{4,12},{5,13},{6,14},{7,15},{8,0},{9,1},... | collective-permute-start | bytes 49160 | tf_op jit(solution)/shard_map/ppermute | solution.py:334
  39.0 2.2 %collective-permute-done.3 = f32[1,4096]{1,0:T(1,128)S(1)} collective-permute-done((f32[1,4096]{1,0:T(1,128)S(1)}, f32[1,4096]{1,0:T(1,128)S(1)}, u32[]{:S(2)}, u32[]{:S(2)}) %collective-permute-start.3) | collective-permute-done | bytes 16416 | tf_op jit(solution)/shard_map/ppermute | solution.py:334
  41.2 0.0 collective-permute-start.12
  41.2 0.0 collective-permute-done.4.refs_1_
  41.2 0.5 %collective-permute-start.10 = (bf16[24,4096]{1,0:T(8,128)(2,1)S(1)}, bf16[24,4096]{1,0:T(8,128)(2,1)S(1)}, u32[]{:S(2)}, u32[]{:S(2)}) collective-permute-start(bf16[24,4096]{1,0:T(8,128)(2,1)S(1)} %collective-permute-done.9.refs_6_), channel_id=1, source_target_pairs={{0,1},{1,0},{2,3},{3,2},{4,5},{5,4},{6,7},{7,6},{8,9},{9,8},{10,11... | collective-permute-start | bytes 589832 | tf_op jit(solution)/shard_map/ppermute | solution.py:334
  41.7 0.0 collective-permute-done.8.refs_5_
  41.7 0.1 collective-permute-start.16
  41.8 0.0 collective-permute-done.6.refs_3_
  41.8 0.4 collective-permute-start.14
  42.2 0.0 collective-permute-done.17.refs_14_
  42.2 0.1 collective-permute-start.18
  42.3 0.3 collective-permute-done.12.refs_9_
  42.6 0.3 collective-permute-done.10.refs_7_
  42.9 0.3 collective-permute-done.16.refs_13_
  43.2 0.3 collective-permute-done.14.refs_11_
  43.5 0.3 collective-permute-done.18.refs_15_
  43.8 0.0 copy-done
  43.8 0.0 copy-done.1
  43.8 3.6 %score.1 = f32[512,384]{1,0:T(8,128)} custom-call(s32[1,4]{1,0:T(1,128)S(1)} %bitcast.2, f32[1,2]{1,0:T(1,128)S(1)} %bitcast.3, f32[1,4096]{1,0:T(1,128)S(1)} %add.15.sums_ref, bf16[512,4096]{1,0:T(8,128)(2,1)S(1)} %get-tuple-element.15.rot_ref, bf16[24,4096]{1,0:T(8,128)(2,1)S(1)} %get-tuple-element.16.refs_0_, ...), custom_call_target="tpu_custom_call" | custom-call | flops 1610612736 | bytes 4194304 | tf_op jit(solution)/shard_map/score/pallas_call | solution.py:301
  (5 shorter events, 0.1 us)
Async XLA Ops:
  1.9 8.0 %collective-permute-start.7 = (bf16[24,4096]{1,0:T(8,128)(2,1)S(1)}, bf16[24,4096]{1,0:T(8,128)(2,1)S(1)}, u32[]{:S(2)}, u32[]{:S(2)}) collective-permute-start(bf16[24,4096]{1,0:T(8,128)(2,1)S(1)} %get-tuple-element.16.refs_0_), channel_id=1, source_target_pairs={{4,0},{5,1},{0,2},{1,3},{8,4},{9,5},{2,6},{3,7},{12,8},{13,9},{6,1... | collective-permute-start | bytes 589832 | tf_op jit(solution)/shard_map/ppermute | solution.py:334
  4.9 6.6 %collective-permute-start.5 = (bf16[24,4096]{1,0:T(8,128)(2,1)S(1)}, bf16[24,4096]{1,0:T(8,128)(2,1)S(1)}, u32[]{:S(2)}, u32[]{:S(2)}) collective-permute-start(bf16[24,4096]{1,0:T(8,128)(2,1)S(1)} %get-tuple-element.16.refs_0_), channel_id=1, source_target_pairs={{2,0},{3,1},{6,2},{7,3},{0,4},{1,5},{10,6},{11,7},{4,8},{5,9},{14,... | collective-permute-start | bytes 589832 | tf_op jit(solution)/shard_map/ppermute | solution.py:334
  9.9 6.1 %collective-permute-start.11 = (bf16[24,4096]{1,0:T(8,128)(2,1)S(1)}, bf16[24,4096]{1,0:T(8,128)(2,1)S(1)}, u32[]{:S(2)}, u32[]{:S(2)}) collective-permute-start(bf16[24,4096]{1,0:T(8,128)(2,1)S(1)} %collective-permute-done.7.refs_4_), channel_id=1, source_target_pairs={{4,0},{5,1},{0,2},{1,3},{8,4},{9,5},{2,6},{3,7},{12,8},{13,9},{6,1... | collective-permute-start | bytes 589832 | tf_op jit(solution)/shard_map/ppermute | solution.py:334
  11.6 5.8 %collective-permute-start.9 = (bf16[24,4096]{1,0:T(8,128)(2,1)S(1)}, bf16[24,4096]{1,0:T(8,128)(2,1)S(1)}, u32[]{:S(2)}, u32[]{:S(2)}) collective-permute-start(bf16[24,4096]{1,0:T(8,128)(2,1)S(1)} %collective-permute-done.5.refs_2_), channel_id=1, source_target_pairs={{2,0},{3,1},{6,2},{7,3},{0,4},{1,5},{10,6},{11,7},{4,8},{5,9},{14,... | collective-permute-start | bytes 589832 | tf_op jit(solution)/shard_map/ppermute | solution.py:334
  15.9 5.7 %collective-permute-start.15 = (bf16[24,4096]{1,0:T(8,128)(2,1)S(1)}, bf16[24,4096]{1,0:T(8,128)(2,1)S(1)}, u32[]{:S(2)}, u32[]{:S(2)}) collective-permute-start(bf16[24,4096]{1,0:T(8,128)(2,1)S(1)} %collective-permute-done.11.refs_8_), channel_id=1, source_target_pairs={{4,0},{5,1},{0,2},{1,3},{8,4},{9,5},{2,6},{3,7},{12,8},{13,9},{6,1... | collective-permute-start | bytes 589832 | tf_op jit(solution)/shard_map/ppermute | solution.py:334
  17.3 5.7 %collective-permute-start.13 = (bf16[24,4096]{1,0:T(8,128)(2,1)S(1)}, bf16[24,4096]{1,0:T(8,128)(2,1)S(1)}, u32[]{:S(2)}, u32[]{:S(2)}) collective-permute-start(bf16[24,4096]{1,0:T(8,128)(2,1)S(1)} %collective-permute-done.9.refs_6_), channel_id=1, source_target_pairs={{2,0},{3,1},{6,2},{7,3},{0,4},{1,5},{10,6},{11,7},{4,8},{5,9},{14,... | collective-permute-start | bytes 589832 | tf_op jit(solution)/shard_map/ppermute | solution.py:334
  18.0 23.2 %collective-permute-start.4 = (bf16[24,4096]{1,0:T(8,128)(2,1)S(1)}, bf16[24,4096]{1,0:T(8,128)(2,1)S(1)}, u32[]{:S(2)}, u32[]{:S(2)}) collective-permute-start(bf16[24,4096]{1,0:T(8,128)(2,1)S(1)} %get-tuple-element.16.refs_0_), channel_id=1, source_target_pairs={{0,1},{1,0},{2,3},{3,2},{4,5},{5,4},{6,7},{7,6},{8,9},{9,8},{10,11... | collective-permute-start | bytes 589832 | tf_op jit(solution)/shard_map/ppermute | solution.py:334
  18.0 23.7 %collective-permute-start.8 = (bf16[24,4096]{1,0:T(8,128)(2,1)S(1)}, bf16[24,4096]{1,0:T(8,128)(2,1)S(1)}, u32[]{:S(2)}, u32[]{:S(2)}) collective-permute-start(bf16[24,4096]{1,0:T(8,128)(2,1)S(1)} %collective-permute-done.7.refs_4_), channel_id=1, source_target_pairs={{0,1},{1,0},{2,3},{3,2},{4,5},{5,4},{6,7},{7,6},{8,9},{9,8},{10,11... | collective-permute-start | bytes 589832 | tf_op jit(solution)/shard_map/ppermute | solution.py:334
  18.5 23.3 %collective-permute-start.6 = (bf16[24,4096]{1,0:T(8,128)(2,1)S(1)}, bf16[24,4096]{1,0:T(8,128)(2,1)S(1)}, u32[]{:S(2)}, u32[]{:S(2)}) collective-permute-start(bf16[24,4096]{1,0:T(8,128)(2,1)S(1)} %collective-permute-done.5.refs_2_), channel_id=1, source_target_pairs={{0,1},{1,0},{2,3},{3,2},{4,5},{5,4},{6,7},{7,6},{8,9},{9,8},{10,11... | collective-permute-start | bytes 589832 | tf_op jit(solution)/shard_map/ppermute | solution.py:334
  23.0 19.2 %collective-permute-start.17 = (bf16[24,4096]{1,0:T(8,128)(2,1)S(1)}, bf16[24,4096]{1,0:T(8,128)(2,1)S(1)}, u32[]{:S(2)}, u32[]{:S(2)}) collective-permute-start(bf16[24,4096]{1,0:T(8,128)(2,1)S(1)} %choose.1), channel_id=1, source_target_pairs={{2,0},{5,1},{6,2},{1,3},{0,4},{9,5},{10,6},{3,7},{4,8},{13,9},{14,... | collective-permute-start | bytes 589832 | tf_op jit(solution)/shard_map/ppermute | solution.py:334
  23.7 20.0 %copy-start = (s32[4]{0:T(128)S(1)}, s32[4]{0:T(128)}, u32[]{:S(2)}) copy-start(s32[4]{0:T(128)} %param.11) | copy-start | bytes 52
  23.7 20.0 %copy-start.1 = (f32[2]{0:T(128)S(1)}, f32[2]{0:T(128)}, u32[]{:S(2)}) copy-start(f32[2]{0:T(128)} %param.10) | copy-start | bytes 28
  27.6 1.2 %collective-permute-start = (f32[1,4096]{1,0:T(1,128)S(1)}, f32[1,4096]{1,0:T(1,128)S(1)}, u32[]{:S(2)}, u32[]{:S(2)}) collective-permute-start(f32[1,4096]{1,0:T(1,128)S(1)} %get-tuple-element.14), channel_id=1, source_target_pairs={{0,1},{1,0},{2,3},{3,2},{4,5},{5,4},{6,7},{7,6},{8,9},{9,8},{10,11... | collective-permute-start | bytes 49160 | tf_op jit(solution)/shard_map/ppermute | solution.py:334
  28.8 3.8 %collective-permute-start.1 = (f32[1,4096]{1,0:T(1,128)S(1)}, f32[1,4096]{1,0:T(1,128)S(1)}, u32[]{:S(2)}, u32[]{:S(2)}) collective-permute-start(f32[1,4096]{1,0:T(1,128)S(1)} %add.12), channel_id=1, source_target_pairs={{0,2},{1,3},{2,0},{3,1},{4,6},{5,7},{6,4},{7,5},{8,10},{9,11},{10,... | collective-permute-start | bytes 49160 | tf_op jit(solution)/shard_map/ppermute | solution.py:334
  32.7 3.8 %collective-permute-start.2 = (f32[1,4096]{1,0:T(1,128)S(1)}, f32[1,4096]{1,0:T(1,128)S(1)}, u32[]{:S(2)}, u32[]{:S(2)}) collective-permute-start(f32[1,4096]{1,0:T(1,128)S(1)} %add.13), channel_id=1, source_target_pairs={{0,4},{1,5},{2,6},{3,7},{4,0},{5,1},{6,2},{7,3},{8,12},{9,13},{10,... | collective-permute-start | bytes 49160 | tf_op jit(solution)/shard_map/ppermute | solution.py:334
  36.5 4.7 %collective-permute-start.3 = (f32[1,4096]{1,0:T(1,128)S(1)}, f32[1,4096]{1,0:T(1,128)S(1)}, u32[]{:S(2)}, u32[]{:S(2)}) collective-permute-start(f32[1,4096]{1,0:T(1,128)S(1)} %add.14), channel_id=1, source_target_pairs={{0,8},{1,9},{2,10},{3,11},{4,12},{5,13},{6,14},{7,15},{8,0},{9,1},... | collective-permute-start | bytes 49160 | tf_op jit(solution)/shard_map/ppermute | solution.py:334
  41.2 1.4 %collective-permute-start.12 = (bf16[24,4096]{1,0:T(8,128)(2,1)S(1)}, bf16[24,4096]{1,0:T(8,128)(2,1)S(1)}, u32[]{:S(2)}, u32[]{:S(2)}) collective-permute-start(bf16[24,4096]{1,0:T(8,128)(2,1)S(1)} %collective-permute-done.11.refs_8_), channel_id=1, source_target_pairs={{0,1},{1,0},{2,3},{3,2},{4,5},{5,4},{6,7},{7,6},{8,9},{9,8},{10,11... | collective-permute-start | bytes 589832 | tf_op jit(solution)/shard_map/ppermute | solution.py:334
  41.2 1.7 %collective-permute-start.10 = (bf16[24,4096]{1,0:T(8,128)(2,1)S(1)}, bf16[24,4096]{1,0:T(8,128)(2,1)S(1)}, u32[]{:S(2)}, u32[]{:S(2)}) collective-permute-start(bf16[24,4096]{1,0:T(8,128)(2,1)S(1)} %collective-permute-done.9.refs_6_), channel_id=1, source_target_pairs={{0,1},{1,0},{2,3},{3,2},{4,5},{5,4},{6,7},{7,6},{8,9},{9,8},{10,11... | collective-permute-start | bytes 589832 | tf_op jit(solution)/shard_map/ppermute | solution.py:334
  41.7 1.5 %collective-permute-start.16 = (bf16[24,4096]{1,0:T(8,128)(2,1)S(1)}, bf16[24,4096]{1,0:T(8,128)(2,1)S(1)}, u32[]{:S(2)}, u32[]{:S(2)}) collective-permute-start(bf16[24,4096]{1,0:T(8,128)(2,1)S(1)} %collective-permute-done.15.odd_ref.refs_12_), channel_id=1, source_target_pairs={{0,1},{1,0},{2,3},{3,2},{4,5},{5,4},{6,7},{7,6},{8,9},{9,8},{10,11... | collective-permute-start | bytes 589832 | tf_op jit(solution)/shard_map/ppermute | solution.py:334
  41.8 1.7 %collective-permute-start.14 = (bf16[24,4096]{1,0:T(8,128)(2,1)S(1)}, bf16[24,4096]{1,0:T(8,128)(2,1)S(1)}, u32[]{:S(2)}, u32[]{:S(2)}) collective-permute-start(bf16[24,4096]{1,0:T(8,128)(2,1)S(1)} %collective-permute-done.13.even_ref.refs_10_), channel_id=1, source_target_pairs={{0,1},{1,0},{2,3},{3,2},{4,5},{5,4},{6,7},{7,6},{8,9},{9,8},{10,11... | collective-permute-start | bytes 589832 | tf_op jit(solution)/shard_map/ppermute | solution.py:334
  42.2 1.5 %collective-permute-start.18 = (bf16[24,4096]{1,0:T(8,128)(2,1)S(1)}, bf16[24,4096]{1,0:T(8,128)(2,1)S(1)}, u32[]{:S(2)}, u32[]{:S(2)}) collective-permute-start(bf16[24,4096]{1,0:T(8,128)(2,1)S(1)} %collective-permute-done.17.refs_14_), channel_id=1, source_target_pairs={{0,1},{1,0},{2,3},{3,2},{4,5},{5,4},{6,7},{7,6},{8,9},{9,8},{10,11... | collective-permute-start | bytes 589832 | tf_op jit(solution)/shard_map/ppermute | solution.py:334

commit v3 on v2

--- a/solution.py
+++ b/solution.py
@@ -157,7 +157,8 @@
     me = lax.axis_index("dp")
     chip, mine = me // 2, me % 2
     spot = jnp.where(chip % 2 == 0, chip // 2, chips - 1 - chip // 2)
-    pieces, score_ref, scaled = refs[:count], refs[count], refs[count + 1 :]
+    pieces, score_ref, scaled = refs[:count], refs[count], refs[count + 1 : -2]
+    held, sems = refs[-2:]
     block = sums_ref.shape[1] // layers
     spots = []
     for step, twin in steps:
@@ -176,27 +177,39 @@
         for where, piece in zip(spots, pieces):
             scaled[slot][pl.ds(where, rows), :] = piece[:, lanes].astype(jnp.float32) * inverse
 
-    def dot(lanes, right):
+    def dot(lanes, right, part=slice(None)):
         return lax.dot_general(
-            rot_ref[:, lanes],
+            rot_ref[part, lanes],
             right.astype(jnp.bfloat16),
             (((1,), (1,)), ((), ())),
             preferred_element_type=jnp.float32,
         )
 
     if len(scaled) == layers:
-        total = None
         for l in range(layers):
             fill(l, slice(l * block, (l + 1) * block), l)
-        for l in range(layers):
-            product = dot(slice(l * block, (l + 1) * block), scaled[l][...])
-            total = product if total is None else total + product
-        score_ref[...] = total
+        own = rot_ref.shape[0]
+        size = own // 2 if own % 32 == 0 else own
+        copies = []
+        for at in range(0, own, size):
+            total = None
+            for l in range(layers):
+                lanes = slice(l * block, (l + 1) * block)
+                product = dot(lanes, scaled[l][...], slice(at, at + size))
+                total = product if total is None else total + product
+            held[at : at + size, :] = total
+            part = pl.ds(at, size)
+            copies.append(
+                pltpu.make_async_copy(held.at[part], score_ref.at[part], sems.at[len(copies)])
+            )
+            copies[-1].start()
+        for copy in copies:
+            copy.wait()
         return
 
     queries = score_ref.shape[1]
     chunk = next(n for n in (512, 384, 256, 128, queries) if queries % n == 0)
-    score_ref[...] = jnp.zeros(score_ref.shape, jnp.float32)
+    held[...] = jnp.zeros(held.shape, jnp.float32)
 
     @pl.loop(0, layers)
     def _(l):
@@ -206,7 +219,11 @@
         @pl.loop(0, queries // chunk)
         def _(n):
             at = pl.ds(pl.multiple_of(n * chunk, chunk), chunk)
-            score_ref[:, at] += dot(lanes, scaled[0][at, :])
+            held[:, at] += dot(lanes, scaled[0][at, :])
+
+    copy = pltpu.make_async_copy(held, score_ref, sems.at[0])
+    copy.start()
+    copy.wait()
 
 
 def prepare(queries, in_basis, out_basis, train, early):
@@ -301,9 +318,10 @@
     return pl.pallas_call(
         functools.partial(score_kernel, layers, steps, rows, train_rows),
         in_specs=[VMEM] * (4 + count),
-        out_specs=VMEM,
+        out_specs=HBM,
         out_shape=jax.ShapeDtypeStruct((own, queries), jnp.float32),
-        scratch_shapes=[pltpu.VMEM((queries, features // layers), jnp.float32)] * slots,
+        scratch_shapes=[pltpu.VMEM((queries, features // layers), jnp.float32)] * slots
+        + [pltpu.VMEM((own, queries), jnp.float32), pltpu.SemaphoreType.DMA((2,))],
         compiler_params=pltpu.CompilerParams(vmem_limit_bytes=max(24 * MIB, need)),
         cost_estimate=pl.CostEstimate(
             flops=2 * own * queries * features, bytes_accessed=2 * own * features, transcendentals=0

time: 47.5 us -> 47.5 us (level)
  no operation moved by 1% of the time
where the time goes in v3:
time: 47.5 us; the launch traced here: 47.4 us
  waiting for transfers between devices  22.8 us (48%)
  starting transfers between devices  15.1 us (32%)
  Pallas kernels  9.32 us (20%)
    ppermute x19, waiting for transfers between devices, send(): return lax.ppermute(x, 'dp', pairs)  22.8 us
    ppermute x19, starting transfers between devices, send(): return lax.ppermute(x, 'dp', pairs)  15.1 us
    pallas_call x1, Pallas kernels, rotate_train(): pl.pallas_call(functools.partial(train_kernel, layers, width, early), in_...  3.83 us
    pallas_call x1, Pallas kernels, score(): pl.pallas_call(functools.partial(score_kernel, layers, steps, rows, train...  3.62 us
    pallas_call x1, Pallas kernels, prepare(): pl.pallas_call(functools.partial(prepare_kernel, layers, width), in_specs...  1.85 us
  transfers between devices with their start and end apart: 19, of which 13 were waited for; matrix products, arithmetic and copies ran while one was open for 0% of the time, Pallas kernels for 8%

profile of v3, /device:TPU:0, one launch (start us, length us, event | category | flops | bytes accessed | tf_op | source)
XLA Modules:
  0.0 47.4 jit_solution(1401656518978026272)
XLA Ops:
  0.0 1.9 %prepare.1 = (bf16[24,4096]{1,0:T(8,128)(2,1)S(1)}, bf16[4,256,256]{2,1,0:T(8,128)(2,1)S(1)}, bf16[4,512,512]{2,1,0:T(8,128)(2,1)S(1)}, bf16[512,2048]{1,0:T(8,128)(2,1)S(1)}) custom-call(bf16[24,4096]{1,0:T(8,128)(2,1)} %q_hbm.1, bf16[4,32,32]{2,1,0:T(8,128)(2,1)} %in_hbm.1, bf16[4,32,32]{2,1,0:T(8,128)(2,1)} %out_hbm.1, bf16[512,4096]{1,0:T(8,128)(2,1)} %x_hbm.3), custom_call_target="tpu_custom_call" | custom-call | flops 805306368 | bytes 4194304 | tf_op jit(solution)/shard_map/prepare/pallas_call | solution.py:234
  1.9 3.0 %collective-permute-start.7 = (bf16[24,4096]{1,0:T(8,128)(2,1)S(1)}, bf16[24,4096]{1,0:T(8,128)(2,1)S(1)}, u32[]{:S(2)}, u32[]{:S(2)}) collective-permute-start(bf16[24,4096]{1,0:T(8,128)(2,1)S(1)} %get-tuple-element.16.refs_0_), channel_id=1, source_target_pairs={{4,0},{5,1},{0,2},{1,3},{8,4},{9,5},{2,6},{3,7},{12,8},{13,9},{6,1... | collective-permute-start | bytes 589832 | tf_op jit(solution)/shard_map/ppermute | solution.py:352
  4.9 0.1 collective-permute-start.5
  5.0 4.8 %collective-permute-done.7.refs_4_ = bf16[24,4096]{1,0:T(8,128)(2,1)S(1)} collective-permute-done((bf16[24,4096]{1,0:T(8,128)(2,1)S(1)}, bf16[24,4096]{1,0:T(8,128)(2,1)S(1)}, u32[]{:S(2)}, u32[]{:S(2)}) %collective-permute-start.7) | collective-permute-done | bytes 196640 | tf_op jit(solution)/shard_map/ppermute | solution.py:352
  9.9 1.7 %collective-permute-start.11 = (bf16[24,4096]{1,0:T(8,128)(2,1)S(1)}, bf16[24,4096]{1,0:T(8,128)(2,1)S(1)}, u32[]{:S(2)}, u32[]{:S(2)}) collective-permute-start(bf16[24,4096]{1,0:T(8,128)(2,1)S(1)} %collective-permute-done.7.refs_4_), channel_id=1, source_target_pairs={{4,0},{5,1},{0,2},{1,3},{8,4},{9,5},{2,6},{3,7},{12,8},{13,9},{6,1... | collective-permute-start | bytes 589832 | tf_op jit(solution)/shard_map/ppermute | solution.py:352
  11.6 0.0 collective-permute-done.5.refs_2_
  11.6 0.3 collective-permute-start.9
  11.9 4.0 %collective-permute-done.11.refs_8_ = bf16[24,4096]{1,0:T(8,128)(2,1)S(1)} collective-permute-done((bf16[24,4096]{1,0:T(8,128)(2,1)S(1)}, bf16[24,4096]{1,0:T(8,128)(2,1)S(1)}, u32[]{:S(2)}, u32[]{:S(2)}) %collective-permute-start.11) | collective-permute-done | bytes 196640 | tf_op jit(solution)/shard_map/ppermute | solution.py:352
  15.9 1.4 %collective-permute-start.15 = (bf16[24,4096]{1,0:T(8,128)(2,1)S(1)}, bf16[24,4096]{1,0:T(8,128)(2,1)S(1)}, u32[]{:S(2)}, u32[]{:S(2)}) collective-permute-start(bf16[24,4096]{1,0:T(8,128)(2,1)S(1)} %collective-permute-done.11.refs_8_), channel_id=1, source_target_pairs={{4,0},{5,1},{0,2},{1,3},{8,4},{9,5},{2,6},{3,7},{12,8},{13,9},{6,1... | collective-permute-start | bytes 589832 | tf_op jit(solution)/shard_map/ppermute | solution.py:352
  17.3 0.0 collective-permute-done.9.refs_6_
  17.3 0.6 %collective-permute-start.13 = (bf16[24,4096]{1,0:T(8,128)(2,1)S(1)}, bf16[24,4096]{1,0:T(8,128)(2,1)S(1)}, u32[]{:S(2)}, u32[]{:S(2)}) collective-permute-start(bf16[24,4096]{1,0:T(8,128)(2,1)S(1)} %collective-permute-done.9.refs_6_), channel_id=1, source_target_pairs={{2,0},{3,1},{6,2},{7,3},{0,4},{1,5},{10,6},{11,7},{4,8},{5,9},{14,... | collective-permute-start | bytes 589832 | tf_op jit(solution)/shard_map/ppermute | solution.py:352
  18.0 0.0 collective-permute-start.4
  18.0 0.5 %collective-permute-start.8 = (bf16[24,4096]{1,0:T(8,128)(2,1)S(1)}, bf16[24,4096]{1,0:T(8,128)(2,1)S(1)}, u32[]{:S(2)}, u32[]{:S(2)}) collective-permute-start(bf16[24,4096]{1,0:T(8,128)(2,1)S(1)} %collective-permute-done.7.refs_4_), channel_id=1, source_target_pairs={{0,1},{1,0},{2,3},{3,2},{4,5},{5,4},{6,7},{7,6},{8,9},{9,8},{10,11... | collective-permute-start | bytes 589832 | tf_op jit(solution)/shard_map/ppermute | solution.py:352
  18.5 0.0 collective-permute-start.6
  18.5 3.1 %collective-permute-done.15.odd_ref.refs_12_ = bf16[24,4096]{1,0:T(8,128)(2,1)S(1)} collective-permute-done((bf16[24,4096]{1,0:T(8,128)(2,1)S(1)}, bf16[24,4096]{1,0:T(8,128)(2,1)S(1)}, u32[]{:S(2)}, u32[]{:S(2)}) %collective-permute-start.15) | collective-permute-done | bytes 196640 | tf_op jit(solution)/shard_map/ppermute | solution.py:352
  21.6 1.4 %collective-permute-done.13.even_ref.refs_10_ = bf16[24,4096]{1,0:T(8,128)(2,1)S(1)} collective-permute-done((bf16[24,4096]{1,0:T(8,128)(2,1)S(1)}, bf16[24,4096]{1,0:T(8,128)(2,1)S(1)}, u32[]{:S(2)}, u32[]{:S(2)}) %collective-permute-start.13) | collective-permute-done | bytes 196640 | tf_op jit(solution)/shard_map/ppermute | solution.py:352
  23.0 0.7 %collective-permute-start.17 = (bf16[24,4096]{1,0:T(8,128)(2,1)S(1)}, bf16[24,4096]{1,0:T(8,128)(2,1)S(1)}, u32[]{:S(2)}, u32[]{:S(2)}) collective-permute-start(bf16[24,4096]{1,0:T(8,128)(2,1)S(1)} %choose.1), channel_id=1, source_target_pairs={{2,0},{5,1},{6,2},{1,3},{0,4},{9,5},{10,6},{3,7},{4,8},{13,9},{14,... | collective-permute-start | bytes 589832 | tf_op jit(solution)/shard_map/ppermute | solution.py:352
  23.7 0.0 copy-start
  23.7 0.0 copy-start.1
  23.7 3.8 %rotate_train.1 = (bf16[512,4096]{1,0:T(8,128)(2,1)S(1)}, f32[1,4096]{1,0:T(1,128)S(1)}) custom-call(bf16[512,4096]{1,0:T(8,128)(2,1)} %x_hbm.3, bf16[512,2048]{1,0:T(8,128)(2,1)S(1)} %get-tuple-element.11.held_ref, bf16[4,256,256]{2,1,0:T(8,128)(2,1)S(1)} %get-tuple-element.12.first_ref, bf16[4,512,512]{2,1,0:T(8,128)(2,1)S(1)} %get-tuple-element.13.second_ref), custom_call_target="tpu_custom_call" | custom-call | flops 3221225472 | bytes 8388608 | tf_op jit(solution)/shard_map/rotate_train/pallas_call | solution.py:264
  27.6 0.1 collective-permute-start
  27.6 1.2 %collective-permute-done = f32[1,4096]{1,0:T(1,128)S(1)} collective-permute-done((f32[1,4096]{1,0:T(1,128)S(1)}, f32[1,4096]{1,0:T(1,128)S(1)}, u32[]{:S(2)}, u32[]{:S(2)}) %collective-permute-start) | collective-permute-done | bytes 16416 | tf_op jit(solution)/shard_map/ppermute | solution.py:352
  28.8 1.5 %collective-permute-start.1 = (f32[1,4096]{1,0:T(1,128)S(1)}, f32[1,4096]{1,0:T(1,128)S(1)}, u32[]{:S(2)}, u32[]{:S(2)}) collective-permute-start(f32[1,4096]{1,0:T(1,128)S(1)} %add.12), channel_id=1, source_target_pairs={{0,2},{1,3},{2,0},{3,1},{4,6},{5,7},{6,4},{7,5},{8,10},{9,11},{10,... | collective-permute-start | bytes 49160 | tf_op jit(solution)/shard_map/ppermute | solution.py:352
  30.3 2.3 %collective-permute-done.1 = f32[1,4096]{1,0:T(1,128)S(1)} collective-permute-done((f32[1,4096]{1,0:T(1,128)S(1)}, f32[1,4096]{1,0:T(1,128)S(1)}, u32[]{:S(2)}, u32[]{:S(2)}) %collective-permute-start.1) | collective-permute-done | bytes 16416 | tf_op jit(solution)/shard_map/ppermute | solution.py:352
  32.7 1.5 %collective-permute-start.2 = (f32[1,4096]{1,0:T(1,128)S(1)}, f32[1,4096]{1,0:T(1,128)S(1)}, u32[]{:S(2)}, u32[]{:S(2)}) collective-permute-start(f32[1,4096]{1,0:T(1,128)S(1)} %add.13), channel_id=1, source_target_pairs={{0,4},{1,5},{2,6},{3,7},{4,0},{5,1},{6,2},{7,3},{8,12},{9,13},{10,... | collective-permute-start | bytes 49160 | tf_op jit(solution)/shard_map/ppermute | solution.py:352
  34.2 2.3 %collective-permute-done.2 = f32[1,4096]{1,0:T(1,128)S(1)} collective-permute-done((f32[1,4096]{1,0:T(1,128)S(1)}, f32[1,4096]{1,0:T(1,128)S(1)}, u32[]{:S(2)}, u32[]{:S(2)}) %collective-permute-start.2) | collective-permute-done | bytes 16416 | tf_op jit(solution)/shard_map/ppermute | solution.py:352
  36.5 2.5 %collective-permute-start.3 = (f32[1,4096]{1,0:T(1,128)S(1)}, f32[1,4096]{1,0:T(1,128)S(1)}, u32[]{:S(2)}, u32[]{:S(2)}) collective-permute-start(f32[1,4096]{1,0:T(1,128)S(1)} %add.14), channel_id=1, source_target_pairs={{0,8},{1,9},{2,10},{3,11},{4,12},{5,13},{6,14},{7,15},{8,0},{9,1},... | collective-permute-start | bytes 49160 | tf_op jit(solution)/shard_map/ppermute | solution.py:352
  39.0 2.2 %collective-permute-done.3 = f32[1,4096]{1,0:T(1,128)S(1)} collective-permute-done((f32[1,4096]{1,0:T(1,128)S(1)}, f32[1,4096]{1,0:T(1,128)S(1)}, u32[]{:S(2)}, u32[]{:S(2)}) %collective-permute-start.3) | collective-permute-done | bytes 16416 | tf_op jit(solution)/shard_map/ppermute | solution.py:352
  41.2 0.0 collective-permute-start.12
  41.2 0.0 collective-permute-done.4.refs_1_
  41.2 0.5 %collective-permute-start.10 = (bf16[24,4096]{1,0:T(8,128)(2,1)S(1)}, bf16[24,4096]{1,0:T(8,128)(2,1)S(1)}, u32[]{:S(2)}, u32[]{:S(2)}) collective-permute-start(bf16[24,4096]{1,0:T(8,128)(2,1)S(1)} %collective-permute-done.9.refs_6_), channel_id=1, source_target_pairs={{0,1},{1,0},{2,3},{3,2},{4,5},{5,4},{6,7},{7,6},{8,9},{9,8},{10,11... | collective-permute-start | bytes 589832 | tf_op jit(solution)/shard_map/ppermute | solution.py:352
  41.7 0.0 collective-permute-done.8.refs_5_
  41.7 0.1 collective-permute-start.16
  41.8 0.0 collective-permute-done.6.refs_3_
  41.8 0.4 collective-permute-start.14
  42.2 0.0 collective-permute-done.17.refs_14_
  42.2 0.1 collective-permute-start.18
  42.3 0.3 collective-permute-done.12.refs_9_
  42.6 0.3 collective-permute-done.10.refs_7_
  42.9 0.3 collective-permute-done.16.refs_13_
  43.2 0.3 collective-permute-done.14.refs_11_
  43.5 0.3 collective-permute-done.18.refs_15_
  43.8 0.0 copy-done
  43.8 0.0 copy-done.1
  43.8 3.6 %score.1 = f32[512,384]{1,0:T(8,128)} custom-call(s32[1,4]{1,0:T(1,128)S(1)} %bitcast.2, f32[1,2]{1,0:T(1,128)S(1)} %bitcast.3, f32[1,4096]{1,0:T(1,128)S(1)} %add.15.sums_ref, bf16[512,4096]{1,0:T(8,128)(2,1)S(1)} %get-tuple-element.15.rot_ref, bf16[24,4096]{1,0:T(8,128)(2,1)S(1)} %get-tuple-element.16.refs_0_, ...), custom_call_target="tpu_custom_call" | custom-call | flops 1610612736 | bytes 4194304 | tf_op jit(solution)/shard_map/score/pallas_call | solution.py:318
  (5 shorter events, 0.1 us)
Async XLA Ops:
  1.9 8.0 %collective-permute-start.7 = (bf16[24,4096]{1,0:T(8,128)(2,1)S(1)}, bf16[24,4096]{1,0:T(8,128)(2,1)S(1)}, u32[]{:S(2)}, u32[]{:S(2)}) collective-permute-start(bf16[24,4096]{1,0:T(8,128)(2,1)S(1)} %get-tuple-element.16.refs_0_), channel_id=1, source_target_pairs={{4,0},{5,1},{0,2},{1,3},{8,4},{9,5},{2,6},{3,7},{12,8},{13,9},{6,1... | collective-permute-start | bytes 589832 | tf_op jit(solution)/shard_map/ppermute | solution.py:352
  4.9 6.6 %collective-permute-start.5 = (bf16[24,4096]{1,0:T(8,128)(2,1)S(1)}, bf16[24,4096]{1,0:T(8,128)(2,1)S(1)}, u32[]{:S(2)}, u32[]{:S(2)}) collective-permute-start(bf16[24,4096]{1,0:T(8,128)(2,1)S(1)} %get-tuple-element.16.refs_0_), channel_id=1, source_target_pairs={{2,0},{3,1},{6,2},{7,3},{0,4},{1,5},{10,6},{11,7},{4,8},{5,9},{14,... | collective-permute-start | bytes 589832 | tf_op jit(solution)/shard_map/ppermute | solution.py:352
  9.9 6.1 %collective-permute-start.11 = (bf16[24,4096]{1,0:T(8,128)(2,1)S(1)}, bf16[24,4096]{1,0:T(8,128)(2,1)S(1)}, u32[]{:S(2)}, u32[]{:S(2)}) collective-permute-start(bf16[24,4096]{1,0:T(8,128)(2,1)S(1)} %collective-permute-done.7.refs_4_), channel_id=1, source_target_pairs={{4,0},{5,1},{0,2},{1,3},{8,4},{9,5},{2,6},{3,7},{12,8},{13,9},{6,1... | collective-permute-start | bytes 589832 | tf_op jit(solution)/shard_map/ppermute | solution.py:352
  11.6 5.8 %collective-permute-start.9 = (bf16[24,4096]{1,0:T(8,128)(2,1)S(1)}, bf16[24,4096]{1,0:T(8,128)(2,1)S(1)}, u32[]{:S(2)}, u32[]{:S(2)}) collective-permute-start(bf16[24,4096]{1,0:T(8,128)(2,1)S(1)} %collective-permute-done.5.refs_2_), channel_id=1, source_target_pairs={{2,0},{3,1},{6,2},{7,3},{0,4},{1,5},{10,6},{11,7},{4,8},{5,9},{14,... | collective-permute-start | bytes 589832 | tf_op jit(solution)/shard_map/ppermute | solution.py:352
  15.9 5.7 %collective-permute-start.15 = (bf16[24,4096]{1,0:T(8,128)(2,1)S(1)}, bf16[24,4096]{1,0:T(8,128)(2,1)S(1)}, u32[]{:S(2)}, u32[]{:S(2)}) collective-permute-start(bf16[24,4096]{1,0:T(8,128)(2,1)S(1)} %collective-permute-done.11.refs_8_), channel_id=1, source_target_pairs={{4,0},{5,1},{0,2},{1,3},{8,4},{9,5},{2,6},{3,7},{12,8},{13,9},{6,1... | collective-permute-start | bytes 589832 | tf_op jit(solution)/shard_map/ppermute | solution.py:352
  17.3 5.7 %collective-permute-start.13 = (bf16[24,4096]{1,0:T(8,128)(2,1)S(1)}, bf16[24,4096]{1,0:T(8,128)(2,1)S(1)}, u32[]{:S(2)}, u32[]{:S(2)}) collective-permute-start(bf16[24,4096]{1,0:T(8,128)(2,1)S(1)} %collective-permute-done.9.refs_6_), channel_id=1, source_target_pairs={{2,0},{3,1},{6,2},{7,3},{0,4},{1,5},{10,6},{11,7},{4,8},{5,9},{14,... | collective-permute-start | bytes 589832 | tf_op jit(solution)/shard_map/ppermute | solution.py:352
  18.0 23.2 %collective-permute-start.4 = (bf16[24,4096]{1,0:T(8,128)(2,1)S(1)}, bf16[24,4096]{1,0:T(8,128)(2,1)S(1)}, u32[]{:S(2)}, u32[]{:S(2)}) collective-permute-start(bf16[24,4096]{1,0:T(8,128)(2,1)S(1)} %get-tuple-element.16.refs_0_), channel_id=1, source_target_pairs={{0,1},{1,0},{2,3},{3,2},{4,5},{5,4},{6,7},{7,6},{8,9},{9,8},{10,11... | collective-permute-start | bytes 589832 | tf_op jit(solution)/shard_map/ppermute | solution.py:352
  18.0 23.7 %collective-permute-start.8 = (bf16[24,4096]{1,0:T(8,128)(2,1)S(1)}, bf16[24,4096]{1,0:T(8,128)(2,1)S(1)}, u32[]{:S(2)}, u32[]{:S(2)}) collective-permute-start(bf16[24,4096]{1,0:T(8,128)(2,1)S(1)} %collective-permute-done.7.refs_4_), channel_id=1, source_target_pairs={{0,1},{1,0},{2,3},{3,2},{4,5},{5,4},{6,7},{7,6},{8,9},{9,8},{10,11... | collective-permute-start | bytes 589832 | tf_op jit(solution)/shard_map/ppermute | solution.py:352
  18.5 23.3 %collective-permute-start.6 = (bf16[24,4096]{1,0:T(8,128)(2,1)S(1)}, bf16[24,4096]{1,0:T(8,128)(2,1)S(1)}, u32[]{:S(2)}, u32[]{:S(2)}) collective-permute-start(bf16[24,4096]{1,0:T(8,128)(2,1)S(1)} %collective-permute-done.5.refs_2_), channel_id=1, source_target_pairs={{0,1},{1,0},{2,3},{3,2},{4,5},{5,4},{6,7},{7,6},{8,9},{9,8},{10,11... | collective-permute-start | bytes 589832 | tf_op jit(solution)/shard_map/ppermute | solution.py:352
  23.0 19.2 %collective-permute-start.17 = (bf16[24,4096]{1,0:T(8,128)(2,1)S(1)}, bf16[24,4096]{1,0:T(8,128)(2,1)S(1)}, u32[]{:S(2)}, u32[]{:S(2)}) collective-permute-start(bf16[24,4096]{1,0:T(8,128)(2,1)S(1)} %choose.1), channel_id=1, source_target_pairs={{2,0},{5,1},{6,2},{1,3},{0,4},{9,5},{10,6},{3,7},{4,8},{13,9},{14,... | collective-permute-start | bytes 589832 | tf_op jit(solution)/shard_map/ppermute | solution.py:352
  23.7 20.0 %copy-start = (s32[4]{0:T(128)S(1)}, s32[4]{0:T(128)}, u32[]{:S(2)}) copy-start(s32[4]{0:T(128)} %param.11) | copy-start | bytes 52
  23.7 20.0 %copy-start.1 = (f32[2]{0:T(128)S(1)}, f32[2]{0:T(128)}, u32[]{:S(2)}) copy-start(f32[2]{0:T(128)} %param.10) | copy-start | bytes 28
  27.6 1.2 %collective-permute-start = (f32[1,4096]{1,0:T(1,128)S(1)}, f32[1,4096]{1,0:T(1,128)S(1)}, u32[]{:S(2)}, u32[]{:S(2)}) collective-permute-start(f32[1,4096]{1,0:T(1,128)S(1)} %get-tuple-element.14), channel_id=1, source_target_pairs={{0,1},{1,0},{2,3},{3,2},{4,5},{5,4},{6,7},{7,6},{8,9},{9,8},{10,11... | collective-permute-start | bytes 49160 | tf_op jit(solution)/shard_map/ppermute | solution.py:352
  28.8 3.8 %collective-permute-start.1 = (f32[1,4096]{1,0:T(1,128)S(1)}, f32[1,4096]{1,0:T(1,128)S(1)}, u32[]{:S(2)}, u32[]{:S(2)}) collective-permute-start(f32[1,4096]{1,0:T(1,128)S(1)} %add.12), channel_id=1, source_target_pairs={{0,2},{1,3},{2,0},{3,1},{4,6},{5,7},{6,4},{7,5},{8,10},{9,11},{10,... | collective-permute-start | bytes 49160 | tf_op jit(solution)/shard_map/ppermute | solution.py:352
  32.7 3.8 %collective-permute-start.2 = (f32[1,4096]{1,0:T(1,128)S(1)}, f32[1,4096]{1,0:T(1,128)S(1)}, u32[]{:S(2)}, u32[]{:S(2)}) collective-permute-start(f32[1,4096]{1,0:T(1,128)S(1)} %add.13), channel_id=1, source_target_pairs={{0,4},{1,5},{2,6},{3,7},{4,0},{5,1},{6,2},{7,3},{8,12},{9,13},{10,... | collective-permute-start | bytes 49160 | tf_op jit(solution)/shard_map/ppermute | solution.py:352
  36.5 4.7 %collective-permute-start.3 = (f32[1,4096]{1,0:T(1,128)S(1)}, f32[1,4096]{1,0:T(1,128)S(1)}, u32[]{:S(2)}, u32[]{:S(2)}) collective-permute-start(f32[1,4096]{1,0:T(1,128)S(1)} %add.14), channel_id=1, source_target_pairs={{0,8},{1,9},{2,10},{3,11},{4,12},{5,13},{6,14},{7,15},{8,0},{9,1},... | collective-permute-start | bytes 49160 | tf_op jit(solution)/shard_map/ppermute | solution.py:352
  41.2 1.4 %collective-permute-start.12 = (bf16[24,4096]{1,0:T(8,128)(2,1)S(1)}, bf16[24,4096]{1,0:T(8,128)(2,1)S(1)}, u32[]{:S(2)}, u32[]{:S(2)}) collective-permute-start(bf16[24,4096]{1,0:T(8,128)(2,1)S(1)} %collective-permute-done.11.refs_8_), channel_id=1, source_target_pairs={{0,1},{1,0},{2,3},{3,2},{4,5},{5,4},{6,7},{7,6},{8,9},{9,8},{10,11... | collective-permute-start | bytes 589832 | tf_op jit(solution)/shard_map/ppermute | solution.py:352
  41.2 1.7 %collective-permute-start.10 = (bf16[24,4096]{1,0:T(8,128)(2,1)S(1)}, bf16[24,4096]{1,0:T(8,128)(2,1)S(1)}, u32[]{:S(2)}, u32[]{:S(2)}) collective-permute-start(bf16[24,4096]{1,0:T(8,128)(2,1)S(1)} %collective-permute-done.9.refs_6_), channel_id=1, source_target_pairs={{0,1},{1,0},{2,3},{3,2},{4,5},{5,4},{6,7},{7,6},{8,9},{9,8},{10,11... | collective-permute-start | bytes 589832 | tf_op jit(solution)/shard_map/ppermute | solution.py:352
  41.7 1.5 %collective-permute-start.16 = (bf16[24,4096]{1,0:T(8,128)(2,1)S(1)}, bf16[24,4096]{1,0:T(8,128)(2,1)S(1)}, u32[]{:S(2)}, u32[]{:S(2)}) collective-permute-start(bf16[24,4096]{1,0:T(8,128)(2,1)S(1)} %collective-permute-done.15.odd_ref.refs_12_), channel_id=1, source_target_pairs={{0,1},{1,0},{2,3},{3,2},{4,5},{5,4},{6,7},{7,6},{8,9},{9,8},{10,11... | collective-permute-start | bytes 589832 | tf_op jit(solution)/shard_map/ppermute | solution.py:352
  41.8 1.7 %collective-permute-start.14 = (bf16[24,4096]{1,0:T(8,128)(2,1)S(1)}, bf16[24,4096]{1,0:T(8,128)(2,1)S(1)}, u32[]{:S(2)}, u32[]{:S(2)}) collective-permute-start(bf16[24,4096]{1,0:T(8,128)(2,1)S(1)} %collective-permute-done.13.even_ref.refs_10_), channel_id=1, source_target_pairs={{0,1},{1,0},{2,3},{3,2},{4,5},{5,4},{6,7},{7,6},{8,9},{9,8},{10,11... | collective-permute-start | bytes 589832 | tf_op jit(solution)/shard_map/ppermute | solution.py:352
  42.2 1.5 %collective-permute-start.18 = (bf16[24,4096]{1,0:T(8,128)(2,1)S(1)}, bf16[24,4096]{1,0:T(8,128)(2,1)S(1)}, u32[]{:S(2)}, u32[]{:S(2)}) collective-permute-start(bf16[24,4096]{1,0:T(8,128)(2,1)S(1)} %collective-permute-done.17.refs_14_), channel_id=1, source_target_pairs={{0,1},{1,0},{2,3},{3,2},{4,5},{5,4},{6,7},{7,6},{8,9},{9,8},{10,11... | collective-permute-start | bytes 589832 | tf_op jit(solution)/shard_map/ppermute | solution.py:352
